TPU v7x, 128 devices: a whole 4x4x4 slice. The times are simulated.
128 devices in a mesh: dp: 1, ep: 128 (over z, y, x, core).
Axes of the slice: x: 4, y: 4, z: 4, core: 2. Of those that a mesh axis runs over, the one named last changes fastest.
Arguments:
- hidden: bfloat16 [2048, 2048], P(('dp', 'ep'))
- k_cache: bfloat16 [2048, 32, 4, 128], P(('dp', 'ep'))
- v_cache: bfloat16 [2048, 32, 4, 128], P(('dp', 'ep'))
- seq_lens: int32 [2048], P(('dp', 'ep'))
- expert_ids: int32 [2048, 8], P(('dp', 'ep'))
- ln_attn: bfloat16 [2048], replicated
- w_q: bfloat16 [2048, 4096], replicated
- w_k: bfloat16 [2048, 512], replicated
- w_v: bfloat16 [2048, 512], replicated
- q_gain: bfloat16 [128], replicated
- k_gain: bfloat16 [128], replicated
- w_o: bfloat16 [4096, 2048], replicated
- ln_moe: bfloat16 [2048], replicated
- w_router: bfloat16 [2048, 128], replicated
- w_gate: bfloat16 [128, 2048, 768], P('ep')
- w_up: bfloat16 [128, 2048, 768], P('ep')
- w_down: bfloat16 [128, 768, 2048], P('ep')
Outputs:
- output 1: bfloat16 [2048, 2048], P(('dp', 'ep'))
- output 2: bfloat16 [2048, 32, 4, 128], P(('dp', 'ep'))
- output 3: bfloat16 [2048, 32, 4, 128], P(('dp', 'ep'))
All inputs are finite; a program needn't handle non-finite values.
Results may differ from a plain program's by a relative error of at most 0.00575958.
Values are sent between devices in bfloat16 or wider.
A program may use at most 1 GiB of HBM per device.

v0:
```python
import jax
import jax.numpy as jnp
from jax import lax
from jax.sharding import PartitionSpec as P

EPS = 1e-6
ROPE_BASE = 1000000.0


def rms_scale(values, gain_vec):
    mean_sq = jnp.mean(values * values, axis=-1, keepdims=True)
    return values * lax.rsqrt(mean_sq + EPS) * gain_vec.astype(jnp.float32)


def rotate_half(values, angles):
    half_dim = values.shape[-1] // 2
    x_low = values[..., :half_dim]
    x_high = values[..., half_dim:]
    cos_val = jnp.cos(angles)
    sin_val = jnp.sin(angles)
    return jnp.concatenate([x_low * cos_val - x_high * sin_val, x_high * cos_val + x_low * sin_val], axis=-1)


def attend(hidden, k_cache, v_cache, seq_lens, ln_attn, w_q, w_k, w_v, q_gain, k_gain, w_o):
    n_seq = hidden.shape[0]
    t_max = k_cache.shape[1]
    head_dim = q_gain.shape[0]
    n_heads = w_q.shape[1] // head_dim
    n_kv = w_k.shape[1] // head_dim
    h_f32 = hidden.astype(jnp.float32)
    x_norm = rms_scale(h_f32, ln_attn).astype(jnp.bfloat16)
    q_proj = jnp.dot(x_norm, w_q, preferred_element_type=jnp.float32).reshape(n_seq, n_heads, head_dim)
    k_proj = jnp.dot(x_norm, w_k, preferred_element_type=jnp.float32).reshape(n_seq, n_kv, head_dim)
    v_new = jnp.dot(x_norm, w_v, preferred_element_type=jnp.float32).astype(jnp.bfloat16).reshape(n_seq, n_kv, head_dim)
    inv_freq = jnp.power(ROPE_BASE, -jnp.arange(0, head_dim, 2).astype(jnp.float32) / head_dim)
    angles = seq_lens.astype(jnp.float32)[:, None, None] * inv_freq[None, None, :]
    q_rot = rotate_half(rms_scale(q_proj, q_gain), angles).astype(jnp.bfloat16)
    k_new = rotate_half(rms_scale(k_proj, k_gain), angles).astype(jnp.bfloat16)
    positions = jnp.arange(t_max, dtype=jnp.int32)
    at_slot = (positions[None, :] == seq_lens[:, None])[:, :, None, None]
    k_all = jnp.where(at_slot, k_new[:, None], k_cache)
    v_all = jnp.where(at_slot, v_new[:, None], v_cache)
    q_grp = q_rot.reshape(n_seq, n_kv, n_heads // n_kv, head_dim)
    scores = jnp.einsum('skgd,stkd->skgt', q_grp, k_all, preferred_element_type=jnp.float32) * (head_dim ** -0.5)
    visible = (positions[None, :] <= seq_lens[:, None])[:, None, None, :]
    scores = jnp.where(visible, scores, -1e30)
    att_probs = jax.nn.softmax(scores, axis=-1).astype(jnp.bfloat16)
    attn_out = jnp.einsum('skgt,stkd->skgd', att_probs, v_all, preferred_element_type=jnp.float32)
    attn_out = attn_out.astype(jnp.bfloat16).reshape(n_seq, n_heads * head_dim)
    y_res = h_f32 + jnp.dot(attn_out, w_o, preferred_element_type=jnp.float32)
    return y_res, k_all, v_all


def route_tables(expert_ids, n_experts, capacity):
    expert_range = jnp.arange(n_experts, dtype=jnp.int32)
    chosen = jnp.any(expert_ids[:, :, None] == expert_range, axis=1)
    chosen_int = chosen.astype(jnp.int32)
    rank_se = jnp.cumsum(chosen_int, axis=0) - chosen_int
    cap_range = jnp.arange(capacity, dtype=jnp.int32)
    send_map = (rank_se.T[:, None, :] == cap_range[None, :, None]) & chosen.T[:, None, :]
    slot_rank = jnp.take_along_axis(rank_se, expert_ids, axis=1)
    slot_ids = expert_ids * capacity + slot_rank
    return send_map.astype(jnp.bfloat16), slot_ids


def solution(mesh):
    n_group = mesh.shape['ep']
    row_spec = P(('dp', 'ep'), None)
    cache_spec = P(('dp', 'ep'), None, None, None)
    len_spec = P(('dp', 'ep'))
    rep_vec = P(None)
    rep_mat = P(None, None)
    exp_spec = P('ep', None, None)

    def local_step(hidden, k_cache, v_cache, seq_lens, expert_ids, ln_attn, w_q, w_k, w_v, q_gain, k_gain, w_o, ln_moe, w_router, w_gate, w_up, w_down):
        y_res, k_all, v_all = attend(hidden, k_cache, v_cache, seq_lens, ln_attn, w_q, w_k, w_v, q_gain, k_gain, w_o)
        r_norm = rms_scale(y_res, ln_moe).astype(jnp.bfloat16)
        logits = jnp.dot(r_norm, w_router, preferred_element_type=jnp.float32)
        gate_vals = jax.nn.softmax(jnp.take_along_axis(logits, expert_ids, axis=1), axis=-1)
        n_seq, n_top = expert_ids.shape
        n_experts = w_router.shape[1]
        n_local = w_gate.shape[0]
        capacity = 2 * n_seq // (n_experts // n_top)
        send_map, slot_ids = route_tables(expert_ids, n_experts, capacity)
        send_rows = jnp.einsum('ecs,sd->ecd', send_map, r_norm, preferred_element_type=jnp.float32).astype(jnp.bfloat16)
        recv_rows = lax.all_to_all(send_rows, 'ep', 0, 0, tiled=True)
        recv_rows = recv_rows.reshape(n_group, n_local, capacity, -1)
        gate_pre = jnp.einsum('secd,edf->secf', recv_rows, w_gate, preferred_element_type=jnp.float32)
        up_pre = jnp.einsum('secd,edf->secf', recv_rows, w_up, preferred_element_type=jnp.float32)
        hidden_act = (jax.nn.silu(gate_pre) * up_pre).astype(jnp.bfloat16)
        out_rows = jnp.einsum('secf,efd->secd', hidden_act, w_down, preferred_element_type=jnp.float32).astype(jnp.bfloat16)
        back_rows = lax.all_to_all(out_rows.reshape(n_group * n_local, capacity, -1), 'ep', 0, 0, tiled=True)
        picked = jnp.take(back_rows.reshape(n_experts * capacity, -1), slot_ids.reshape(-1), axis=0)
        picked = picked.reshape(n_seq, n_top, -1).astype(jnp.float32)
        moe_out = jnp.sum(gate_vals[:, :, None] * picked, axis=1)
        return (y_res + moe_out).astype(jnp.bfloat16), k_all, v_all

    return jax.shard_map(local_step, mesh=mesh, in_specs=(row_spec, cache_spec, cache_spec, len_spec, row_spec, rep_vec, rep_mat, rep_mat, rep_mat, rep_vec, rep_vec, rep_mat, rep_vec, rep_mat, exp_spec, exp_spec, exp_spec), out_specs=(row_spec, cache_spec, cache_spec), check_vma=False)
```

profile of v0, /device:TPU:1, one launch (start us, length us, event | category | flops | bytes accessed | tf_op | source)
XLA Modules:
  0.0 111.7 jit_solution(8620284892934388165)
XLA Ops:
  0.6 0.0 copy-start
  0.6 0.0 copy-start.2
  0.7 0.8 convert_element_type.76
  1.5 0.9 iota_compare_fusion.3
  2.4 0.7 convert_element_type.73
  3.0 1.0 fusion.37
  4.0 2.1 %fusion.62 = f32[16,512]{1,0:T(8,128)S(1)} fusion(bf16[2048,512]{1,0:T(8,128)(2,1)} %param.24, bf16[16,2048]{1,0:T(8,128)(2,1)} %param.17, f32[2048]{0:T(1024)S(1)} %convert_element_type.73, f32[16]{0:T(128)S(1)} %add_rsqrt_fusion.3), kind=kOutput, calls=%fused_computation.95 | convolution fusion | flops 33685504 | bytes 2203712 | tf_op jit(solution)/shard_map/dot_general | solution.py:33
  6.1 0.1 multiply_reduce_fusion.3
  6.2 0.7 convert_element_type.78
  6.9 2.0 %convolution_convert_fusion.2 = bf16[16,512]{1,0:T(8,128)(2,1)S(1)} fusion(bf16[2048,512]{1,0:T(8,128)(2,1)} %param.25, bf16[16,2048]{1,0:T(8,128)(2,1)} %param.17, f32[2048]{0:T(1024)S(1)} %convert_element_type.73, f32[16]{0:T(128)S(1)} %add_rsqrt_fusion.3), kind=kOutput, calls=%fused_computation.24 | convolution fusion | flops 33693696 | bytes 2187328 | tf_op jit(solution)/shard_map/dot_general | solution.py:34
  8.9 0.0 copy-done.2
  9.0 0.0 copy-start.8
  9.0 0.0 copy-start.4
  9.0 0.0 copy-start.5
  9.0 8.2 %convolution_bitcast_fusion = f32[2,8,32,128]{3,1,2,0:T(8,128)S(1)} fusion(bf16[2048,4096]{1,0:T(8,128)(2,1)} %param.23, bf16[16,2048]{1,0:T(8,128)(2,1)S(1)} %copy-done.2, f32[2048]{0:T(1024)S(1)} %convert_element_type.73, f32[16]{0:T(128)S(1)} %add_rsqrt_fusion.3), kind=kOutput, calls=%fused_computation.20 | convolution fusion | flops 268566528 | bytes 17113152 | tf_op jit(solution)/shard_map/dot_general | solution.py:32
  17.2 0.1 copy.65
  17.2 0.1 multiply_reduce_fusion.1
  17.4 0.0 copy-done.8
  17.4 0.1 multiply_multiply_fusion.1
  17.5 0.1 multiply_cosine_fusion
  17.6 0.1 multiply_multiply_fusion
  17.8 0.1 subtract_convert_fusion.1
  17.9 0.1 fusion.40
  18.0 0.1 pad_maximum_fusion
  18.1 0.0 copy-done.4
  18.1 0.0 copy-done.5
  18.1 1.5 %broadcast_select_fusion.1 = (bf16[16,32,4,128]{3,2,1,0:T(4,128)(2,1)S(1)}, bf16[16,32,4,128]{3,2,1,0:T(4,128)(2,1)}) fusion(bf16[16,32,4,128]{3,2,1,0:T(4,128)(2,1)S(1)} %copy-done.4, pred[16,32]{1,0:T(8,128)(4,1)S(1)} %get-tuple-element.15, bf16[16,4,128]{2,1,0:T(4,128)(2,1)S(1)} %pad_maximum_fusion, bf16[16,32,4,128]{3,2,1,0:T(4,128)(2,1)S(1)} %copy-done.5, ...), kind=kLoop, calls=%fused_computation.32 | loop fusion | flops 524288 | bytes 2130432 | tf_op jit(solution)/shard_map/jit(_where)/select_n | solution.py:41
  19.6 0.8 copy-done.1
  20.4 0.4 fusion.26
  20.8 0.7 copy-done.3
  21.5 0.3 fusion.65
  21.8 2.2 %convolution_convert_fusion.1 = bf16[16,4,8,128]{3,2,1,0:T(8,128)(2,1)S(1)} fusion(bf16[16,32,4,128]{3,2,1,0:T(4,128)(2,1)} %get-tuple-element.11, f32[16,4,8]{2,1,0:T(4,128)S(1)} %fusion.65, f32[16,4,8,32]{3,2,1,0:T(8,128)} %copy-done.3), kind=kOutput, calls=%fused_computation.23 | convolution fusion | flops 4309535 | bytes 722944 | tf_op jit(solution)/shard_map/skgt,stkd->skgd/dot_general | solution.py:48
  24.0 8.2 %multiply_reduce_fusion.2 = (f32[16]{0:T(128)S(1)}, f32[16,2048]{1,0:T(8,128)S(1)}) fusion(bf16[4096,2048]{1,0:T(8,128)(2,1)} %param.28, bf16[2,8,32,128]{3,2,1,0:T(8,128)(2,1)S(1)} %bitcast.90, bf16[16,2048]{1,0:T(8,128)(2,1)S(1)} %copy-done.2), kind=kOutput, calls=%fused_computation.53 | convolution fusion | flops 268566528 | bytes 17104960 | tf_op jit(solution)/shard_map/dot_general | solution.py:50
  32.2 0.0 copy-done.7
  32.2 0.0 copy-done.6
  32.2 0.1 copy.57
  32.3 0.1 fusion.49
  32.5 0.5 convolution_convert_fusion
  33.0 2.1 %copy.60 = bf16[128,2,2048]{2,1,0:T(2,128)(2,1)} copy(bf16[128,2,2048]{2,0,1:T(8,128)(2,1)S(1)} %convolution_convert_fusion) | data formatting | bytes 2097152 | tf_op jit(solution)/shard_map/convert_element_type | solution.py:85
  35.1 12.0 %all-to-all-start = ((bf16[128,2,2048]{2,1,0:T(2,128)(2,1)}), bf16[128,2,2048]{2,1,0:T(2,128)(2,1)}, u32[]{:S(2)}, u32[]{:S(2)}) async-start(bf16[128,2,2048]{2,1,0:T(2,128)(2,1)} %copy.60), calls=%async_computation | async-start | bytes 2097152 | tf_op jit(solution)/shard_map/all_to_all | solution.py:86
  47.1 1.3 %fusion.60 = f32[16,128]{1,0:T(8,128)S(1)} fusion(bf16[2048,128]{1,0:T(8,128)(2,1)} %param.30, f32[16,2048]{1,0:T(8,128)S(1)} %get-tuple-element.17, f32[2048]{0:T(1024)S(1)} %convert_element_type.82, f32[16]{0:T(128)S(1)} %add_rsqrt_fusion.2), kind=kOutput, calls=%fused_computation.94 | convolution fusion | flops 8486912 | bytes 671808 | tf_op jit(solution)/shard_map/dot_general | solution.py:78
  48.3 17.4 %all-to-all-done = bf16[128,2,2048]{2,1,0:T(2,128)(2,1)} async-done(((bf16[128,2,2048]{2,1,0:T(2,128)(2,1)}), bf16[128,2,2048]{2,1,0:T(2,128)(2,1)}, u32[]{:S(2)}, u32[]{:S(2)}) %all-to-all-start) | async-done | bytes 1048608 | tf_op jit(solution)/shard_map/all_to_all | solution.py:86
  65.7 4.5 %fusion.10 = f32[128,1,2,768]{3,0,2,1:T(8,128)} fusion(bf16[1,2048,768]{2,1,0:T(8,128)(2,1)} %param.31, bf16[128,2,2048]{2,1,0:T(2,128)(2,1)} %all-to-all-done), kind=kOutput, calls=%fused_computation.13 | convolution fusion | flops 805306368 | bytes 4980736 | tf_op jit(solution)/shard_map/secd,edf->secf/dot_general | solution.py:88
  70.2 0.0 copy-done
  70.2 5.7 %fusion.7 = bf16[128,2,2048]{2,0,1:T(8,128)(2,1)} fusion(bf16[1,768,2048]{2,1,0:T(8,128)(2,1)S(1)} %copy-done, bf16[1,2048,768]{2,1,0:T(8,128)(2,1)} %param.32, bf16[128,2,2048]{2,1,0:T(2,128)(2,1)} %all-to-all-done, f32[128,1,2,768]{3,0,2,1:T(8,128)} %fusion.10), kind=kOutput, calls=%fused_computation.11 | convolution fusion | flops 1612316672 | bytes 9175040 | tf_op jit(solution)/shard_map/secf,efd->secd/dot_general | solution.py:91
  75.8 3.3 %copy.63 = bf16[128,2,2048]{2,1,0:T(2,128)(2,1)} copy(bf16[128,2,2048]{2,0,1:T(8,128)(2,1)} %fusion.7) | data formatting | bytes 2097152 | tf_op jit(solution)/shard_map/convert_element_type | solution.py:91
  79.1 5.3 %all-to-all-start.1 = ((bf16[128,2,2048]{2,1,0:T(2,128)(2,1)}), bf16[128,2,2048]{2,1,0:T(2,128)(2,1)}, u32[]{:S(2)}, u32[]{:S(2)}) async-start(bf16[128,2,2048]{2,1,0:T(2,128)(2,1)} %copy.63), calls=%async_computation.1 | async-start | bytes 2097152 | tf_op jit(solution)/shard_map/all_to_all | solution.py:92
  84.5 0.1 copy.54
  84.5 0.1 reshape.292
  84.6 1.2 %gather_fusion.1 = f32[128]{0:T(128)S(1)} fusion(f32[16,128]{1,0:T(8,128)S(1)} %fusion.60, s32[128]{0:T(128)S(1)} %reshape.292), kind=kCustom, calls=%fused_computation.1 | custom fusion | bytes 2048 | tf_op jit(solution)/shard_map/jit(take_along_axis)/gather | solution.py:79
  85.9 0.1 reshape.295
  86.0 0.1 copy.55
  86.0 1.3 %gather_fusion.2 = s32[128]{0:T(128)S(1)} fusion(s32[16,128]{1,0:T(8,128)S(1)} %convert_subtract_fusion, s32[128]{0:T(128)S(1)} %reshape.292), kind=kCustom, calls=%fused_computation.2 | custom fusion | bytes 2048 | tf_op jit(solution)/shard_map/jit(take_along_axis)/gather | solution.py:61
  87.3 0.1 reshape.301
  87.4 0.1 copy.58
  87.5 0.1 copy.56
  87.6 0.1 copy.64
  87.7 0.1 reshape.283
  87.8 0.1 copy.59
  87.9 15.4 %all-to-all-done.1 = bf16[128,2,2048]{2,1,0:T(2,128)(2,1)} async-done(((bf16[128,2,2048]{2,1,0:T(2,128)(2,1)}), bf16[128,2,2048]{2,1,0:T(2,128)(2,1)}, u32[]{:S(2)}, u32[]{:S(2)}) %all-to-all-start.1) | async-done | bytes 1048608 | tf_op jit(solution)/shard_map/all_to_all | solution.py:92
  103.3 2.3 %reshape.282 = bf16[256,2048]{1,0:T(8,128)(2,1)} reshape(bf16[128,2,2048]{2,1,0:T(2,128)(2,1)} %all-to-all-done.1) | data formatting | bytes 2097152 | tf_op jit(solution)/shard_map/reshape | solution.py:93
  105.5 3.6 %gather_fusion = bf16[128,2048]{1,0:T(8,128)(2,1)} fusion(bf16[256,2048]{1,0:T(8,128)(2,1)} %reshape.282, s32[1024]{0:T(1024)S(1)} %pad_clamp_fusion), kind=kCustom, calls=%fused_computation | custom fusion | bytes 1049088 | tf_op jit(solution)/shard_map/jit(_take)/gather | solution.py:93
  109.1 2.0 %multiply_reduce_fusion = f32[16,2048]{1,0:T(8,128)S(1)} fusion(bf16[128,2048]{1,0:T(8,128)(2,1)} %gather_fusion, f32[16,8]{1,0:T(8,128)S(1)} %copy.56, pred[16,8]{1,0:T(8,128)(4,1)S(1)} %copy.59), kind=kLoop, calls=%fused_computation.25 | loop fusion | flops 1015808 | bytes 656000 | tf_op jit(solution)/shard_map/reduce_sum | solution.py:95
  111.1 0.6 add_convert_fusion.1
  (24 shorter events, 0.2 us)
Async XLA Ops:
  0.6 69.5 %copy-start = (bf16[1,768,2048]{2,1,0:T(8,128)(2,1)S(1)}, bf16[1,768,2048]{2,1,0:T(8,128)(2,1)}, u32[]{:S(2)}) copy-start(bf16[1,768,2048]{2,1,0:T(8,128)(2,1)} %param.33) | copy-start | bytes 9437188
  0.6 8.3 %copy-start.2 = (bf16[16,2048]{1,0:T(8,128)(2,1)S(1)}, bf16[16,2048]{1,0:T(8,128)(2,1)}, u32[]{:S(2)}) copy-start(bf16[16,2048]{1,0:T(8,128)(2,1)} %param.17) | copy-start | bytes 196612
  9.0 8.4 %copy-start.8 = (bf16[128]{0:T(256)(128)(2,1)S(1)}, bf16[128]{0:T(256)(128)(2,1)}, u32[]{:S(2)}) copy-start(bf16[128]{0:T(256)(128)(2,1)} %param.26) | copy-start | bytes 772
  9.0 9.1 %copy-start.4 = (bf16[16,32,4,128]{3,2,1,0:T(4,128)(2,1)S(1)}, bf16[16,32,4,128]{3,2,1,0:T(4,128)(2,1)}, u32[]{:S(2)}) copy-start(bf16[16,32,4,128]{3,2,1,0:T(4,128)(2,1)} %param.18) | copy-start | bytes 1572868
  9.0 9.1 %copy-start.5 = (bf16[16,32,4,128]{3,2,1,0:T(4,128)(2,1)S(1)}, bf16[16,32,4,128]{3,2,1,0:T(4,128)(2,1)}, u32[]{:S(2)}) copy-start(bf16[16,32,4,128]{3,2,1,0:T(4,128)(2,1)} %param.19) | copy-start | bytes 1572868
  19.6 0.8 copy-start.1
  20.8 0.7 copy-start.3
  24.0 8.2 %copy-start.7 = (bf16[2048]{0:T(1024)(128)(2,1)S(1)}, bf16[2048]{0:T(1024)(128)(2,1)}, u32[]{:S(2)}) copy-start(bf16[2048]{0:T(1024)(128)(2,1)} %param.29) | copy-start | bytes 12292
  24.0 8.2 %copy-start.6 = (s32[16,8]{0,1:T(8,128)S(1)}, s32[16,8]{0,1:T(8,128)}, u32[]{:S(2)}) copy-start(s32[16,8]{0,1:T(8,128)} %param.21) | copy-start | bytes 1540
  35.1 30.6 %all-to-all-start = ((bf16[128,2,2048]{2,1,0:T(2,128)(2,1)}), bf16[128,2,2048]{2,1,0:T(2,128)(2,1)}, u32[]{:S(2)}, u32[]{:S(2)}) async-start(bf16[128,2,2048]{2,1,0:T(2,128)(2,1)} %copy.60), calls=%async_computation | async-start | bytes 2097152 | tf_op jit(solution)/shard_map/all_to_all | solution.py:86
  79.1 24.1 %all-to-all-start.1 = ((bf16[128,2,2048]{2,1,0:T(2,128)(2,1)}), bf16[128,2,2048]{2,1,0:T(2,128)(2,1)}, u32[]{:S(2)}, u32[]{:S(2)}) async-start(bf16[128,2,2048]{2,1,0:T(2,128)(2,1)} %copy.63), calls=%async_computation.1 | async-start | bytes 2097152 | tf_op jit(solution)/shard_map/all_to_all | solution.py:92
where the time goes:
time: 112 us
  matrix products  35 us (31%)
  waiting for transfers between devices  32.7 us (29%)
  starting transfers between devices  17.3 us (15%)
  local copies, waits for them, and re-layouts  16.2 us (14%)
  other arithmetic  9.49 us (8%)
    all_to_all x1, waiting for transfers between devices, local_step(): recv_rows = lax.all_to_all(send_rows, 'ep', 0, 0, tiled=True)  17.4 us
    all_to_all x1, waiting for transfers between devices, local_step(): lax.all_to_all(out_rows.reshape(n_group * n_local, capacity, -1), 'ep', 0...  15.4 us
    all_to_all x1, starting transfers between devices, local_step(): recv_rows = lax.all_to_all(send_rows, 'ep', 0, 0, tiled=True)  12 us
    dot_general x1, matrix products, attend(): y_res = h_f32 + jnp.dot(attn_out, w_o, preferred_element_type=jnp.float32)  8.2 us
    dot_general x1, matrix products, attend(): jnp.dot(x_norm, w_q, preferred_element_type=jnp.float32)  8.18 us
    dot_general x1, matrix products, local_step(): jnp.einsum('secf,efd->secd', hidden_act, w_down, preferred_element_type=j...  5.65 us
    all_to_all x1, starting transfers between devices, local_step(): lax.all_to_all(out_rows.reshape(n_group * n_local, capacity, -1), 'ep', 0...  5.33 us
    dot_general x1, matrix products, local_step(): jnp.einsum('secd,edf->secf', recv_rows, w_gate, preferred_element_type=jn...  4.48 us
  transfers between devices with their start and end apart: 2, of which 2 were waited for; matrix products, arithmetic and copies ran while one was open for 4% of the time, Pallas kernels for 0%

commit v1 on v0

v1 whole, which is shorter than its diff:
```python
import functools

import jax
import jax.numpy as jnp
import numpy as np
from jax import lax
from jax.experimental import pallas as pl
from jax.experimental.pallas import tpu as pltpu
from jax.sharding import PartitionSpec as P

MESH = pl.DeviceIdType.MESH
EPS = 1e-6
ROPE_BASE = 1000000.0
BF = jnp.bfloat16
F32 = jnp.float32
N = 128
S = 16
D = 2048
HD = 128
T = 32
NKV = 4
GQ = 8
FF = 768
CAP = 2
MIX = 37
GRP = 2


def offset_of(k):
    return (k * MIX) % N


def shift_dev(me, off, sign):
    c = (me % 2 + off) % 2
    x = (me // 2 % 4 + 4 + sign * (off // 2 % 4)) % 4
    y = (me // 8 % 4 + 4 + sign * (off // 8 % 4)) % 4
    z = (me // 32 + 4 + sign * (off // 32)) % 4
    return ((z * 4 + y) * 4 + x) * 2 + c


def rms_rope(v, gain, cos, sin):
    ms = jnp.mean(v * v, axis=-1, keepdims=True)
    v = v * lax.rsqrt(ms + EPS) * gain
    return v * cos + pltpu.roll(v, 64, axis=1) * sin


def kernel(h_hbm, kc_hbm, vc_hbm, sl_hbm, ids_hbm, lna_hbm, wq_hbm, wk_hbm, wv_hbm, qg_hbm, kg_hbm, wo_hbm,
           lnm_hbm, wr_hbm, wg_hbm, wu_hbm, wd_hbm, freq_hbm,
           out_ref, ko_hbm, vo_hbm,
           h_v, sl_s, ids_v, lna_v, lnm_v, qg_v, kg_v, freq_v,
           wk_v, wv_v, wq_v, wo_v, wr_v, wg_v, wu_v, wd_v,
           kc_v, vc_v, kp_v, vp_v, x_v, kn_v, mask_v, trig_v, at_v, y_v, r_v, p_v, snd_v, g_v, hid_v,
           sbuf, rbuf, obuf, bbuf,
           sm_small, sm_kv, sm_cache, sm_wq, sm_wo, sm_wr, sm_we, sm_out,
           ssem, osem, rsem, bsem):
    me = lax.axis_index("ep")
    cp = pltpu.make_async_copy

    small = [cp(a, b, sm_small.at[i]) for i, (a, b) in enumerate([
        (h_hbm, h_v), (lna_hbm, lna_v), (sl_hbm, sl_s), (freq_hbm, freq_v), (kg_hbm, kg_v), (qg_hbm, qg_v),
        (ids_hbm, ids_v), (lnm_hbm, lnm_v)])]
    for c in small:
        c.start()
    kvw = [cp(wk_hbm, wk_v, sm_kv.at[0]), cp(wv_hbm, wv_v, sm_kv.at[1])]
    caches = [cp(kc_hbm, kc_v, sm_cache.at[0]), cp(vc_hbm, vc_v, sm_cache.at[1])]

    def wq_copy(g):
        return cp(wq_hbm.at[:, pl.ds(pl.multiple_of(g * 1024, 1024), 1024)], wq_v.at[g], sm_wq.at[g])

    def wo_copy(n):
        return cp(wo_hbm.at[:, pl.ds(pl.multiple_of(n * 512, 512), 512)], wo_v.at[n], sm_wo.at[n])

    for c in kvw + caches:
        c.start()
    wq_copy(0).start()
    wq_copy(1).start()

    bar = pltpu.get_barrier_semaphore()

    @pl.loop(1, N)
    def _(k):
        pl.semaphore_signal(bar, inc=1, device_id={"ep": (me + k) % N}, device_id_type=MESH)

    for c in small:
        c.wait()

    lane = lax.broadcasted_iota(jnp.int32, (S, CAP * N), 1)
    off = ((lane >> 1) * MIX) & (N - 1)
    mc, mx, my, mz = me % 2, me // 2 % 4, me // 8 % 4, me // 32
    e_row = (((((mz + (off >> 5)) & 3) * 4 + ((my + ((off >> 3) & 3)) & 3)) * 4 + ((mx + ((off >> 1) & 3)) & 3)) * 2
             + ((mc + (off & 1)) & 1))
    ids = ids_v[...]
    chosen = jnp.zeros((S, CAP * N), F32)
    for k in range(8):
        chosen = chosen + jnp.where(ids[:, k:k + 1] == e_row, 1.0, 0.0)
    tri = jnp.where(lax.broadcasted_iota(jnp.int32, (S, S), 0) > lax.broadcasted_iota(jnp.int32, (S, S), 1), 1.0, 0.0)
    rank = jnp.dot(tri.astype(BF), chosen.astype(BF), preferred_element_type=F32)
    send = chosen * jnp.where(rank == (lane & 1).astype(F32), 1.0, 0.0)
    snd_v[...] = send
    p_v[...] = jnp.transpose(send).astype(BF)

    hf = h_v[...].astype(F32)
    rs = lax.rsqrt(jnp.mean(hf * hf, axis=-1, keepdims=True) + EPS)
    lna = lna_v[...].astype(F32)
    for j in range(16):
        sl = slice(j * 128, (j + 1) * 128)
        x_v[:, sl] = (hf[:, sl] * rs * lna[j:j + 1, :]).astype(BF)

    srow = lax.broadcasted_iota(jnp.int32, (S, 128), 0)
    lens = jnp.zeros((S, 128), jnp.int32)
    for s in range(S):
        lens = jnp.where(srow == s, sl_s[s], lens)
    ang = lens.astype(F32) * freq_v[...]
    sgn = jnp.where(lax.broadcasted_iota(jnp.int32, (S, 128), 1) < 64, -1.0, 1.0)
    cos = jnp.cos(ang)
    sin = jnp.sin(ang) * sgn
    trig_v[0] = cos
    trig_v[1] = sin
    for b in range(4):
        col = lax.broadcasted_iota(jnp.int32, (S, 128), 1) + b * 128
        ok = ((col >> 5) == srow) & ((col & 31) <= lens)
        mask_v[:, b * 128:(b + 1) * 128] = jnp.where(ok, 0.0, -1e30)

    x = x_v[...]
    kg = kg_v[...].astype(F32)
    kvw[0].wait()
    kp = jnp.dot(x, wk_v[...], preferred_element_type=F32)
    for g in range(NKV):
        kn_v[0, g] = rms_rope(kp[:, g * 128:(g + 1) * 128], kg, cos, sin)
    kvw[1].wait()
    vp = jnp.dot(x, wv_v[...], preferred_element_type=F32)
    for g in range(NKV):
        kn_v[1, g] = vp[:, g * 128:(g + 1) * 128]

    ri = lax.broadcasted_iota(jnp.int32, (256, 64), 0)
    ci = lax.broadcasted_iota(jnp.int32, (256, 64), 1)
    rep1 = jnp.where(((ri >> 4) == (ci & 15)) & ((ri & 3) == (ci >> 4)), 1.0, 0.0).astype(BF)
    pr = lax.broadcasted_iota(jnp.int32, (128, 128), 0)
    pc = lax.broadcasted_iota(jnp.int32, (128, 128), 1)
    perm = jnp.where(((pr & 31) == (pc >> 2)) & ((pr >> 5) == (pc & 3)), 1.0, 0.0).astype(BF)
    trow = pr >> 2
    for i, (buf, dst) in enumerate(((kc_v, kp_v), (vc_v, vp_v))):
        caches[i].wait()
        rows = buf.reshape(S * T * NKV, HD)
        new = jnp.concatenate([kn_v[i, g].astype(BF) for g in range(NKV)], axis=0)
        rep = jnp.dot(rep1, new, preferred_element_type=F32)
        for s in range(S):
            old = rows[s * 128:(s + 1) * 128, :].astype(F32)
            rep_s = jnp.concatenate([rep[s * 16:(s + 1) * 16, :]] * 8, axis=0)
            upd = jnp.where(trow == sl_s[s], rep_s, old).astype(BF)
            rows[s * 128:(s + 1) * 128, :] = upd
            grp = jnp.dot(perm, upd, preferred_element_type=F32).astype(BF)
            for g in range(NKV):
                dst[g, s * 32:(s + 1) * 32, :] = grp[g * 32:(g + 1) * 32, :]
    couts = [cp(kc_v, ko_hbm, sm_out.at[0]), cp(vc_v, vo_hbm, sm_out.at[1])]

    qg = qg_v[...].astype(F32)

    @pl.loop(0, NKV)
    def _(g):
        wq_copy(g).wait()

        @pl.when(g < 2)
        def _():
            wq_copy(g + 2).start()

        @pl.when(g >= 2)
        def _():
            wo_copy(g - 2).start()
        q = jnp.dot(x_v[...], wq_v[g], preferred_element_type=F32)
        q = jnp.concatenate([q[:, j * 128:(j + 1) * 128] for j in range(GQ)], axis=0)
        cs = jnp.concatenate([trig_v[0]] * GQ, axis=0)
        sn = jnp.concatenate([trig_v[1]] * GQ, axis=0)
        q = rms_rope(q, qg, cs, sn).astype(BF)
        sc = lax.dot_general(q, kp_v[g], (((1,), (1,)), ((), ())), preferred_element_type=F32)
        mk = mask_v[...]
        sc = jnp.where(jnp.concatenate([mk] * GQ, axis=0) == 0.0, sc * (HD ** -0.5), -1e30)
        ex = jnp.exp(sc - jnp.max(sc, axis=-1, keepdims=True))
        pb = (ex / jnp.sum(ex, axis=-1, keepdims=True)).astype(BF)
        o = jnp.dot(pb, vp_v[g], preferred_element_type=F32).astype(BF)
        for j in range(GQ):
            at_v[:, pl.ds(pl.multiple_of((g * GQ + j) * 128, 128), 128)] = o[j * S:(j + 1) * S, :]

    for c in couts:
        c.start()
    wr_c = cp(wr_hbm, wr_v, sm_wr)
    we_c = [cp(wg_hbm.at[0], wg_v, sm_we.at[0]), cp(wu_hbm.at[0], wu_v, sm_we.at[1]), cp(wd_hbm.at[0], wd_v, sm_we.at[2])]

    @pl.loop(0, 4)
    def _(n):
        wo_copy(n).wait()

        @pl.when(n < 2)
        def _():
            wo_copy(n + 2).start()

        @pl.when(n == 2)
        def _():
            wr_c.start()
            we_c[0].start()

        @pl.when(n == 3)
        def _():
            we_c[1].start()
            we_c[2].start()
        cols = pl.ds(pl.multiple_of(n * 512, 512), 512)
        y_v[:, cols] = h_v[:, cols].astype(F32) + jnp.dot(at_v[...], wo_v[n], preferred_element_type=F32)

    y = y_v[...]
    rs = lax.rsqrt(jnp.mean(y * y, axis=-1, keepdims=True) + EPS)
    lnm = lnm_v[...].astype(F32)
    for j in range(16):
        sl = slice(j * 128, (j + 1) * 128)
        r_v[:, sl] = (y[:, sl] * rs * lnm[j:j + 1, :]).astype(BF)

    sview, rview = sbuf.reshape(16, CAP * N, HD), rbuf.reshape(16, CAP * N, HD)
    oview, bview = obuf.reshape(16, CAP * N, HD), bbuf.reshape(16, CAP * N, HD)
    for n in range(4):
        rows = jnp.dot(p_v[...], r_v[:, n * 512:(n + 1) * 512], preferred_element_type=F32).astype(BF)
        for j in range(4):
            sview[n * 4 + j] = rows[:, j * 128:(j + 1) * 128]
    pl.semaphore_wait(bar, N - 1)
    gsz = N // GRP
    for q in range(GRP):
        @pl.loop(1 if q == 0 else q * gsz, (q + 1) * gsz)
        def _(k):
            pltpu.make_async_remote_copy(sbuf.at[:, k], rbuf.at[:, k], ssem, rsem.at[q],
                                         device_id={"ep": shift_dev(me, offset_of(k), 1)}, device_id_type=MESH).start()
    rbuf[:, 0] = sbuf[:, 0]

    wr_c.wait()
    logits = jnp.dot(r_v[...], wr_v[...], preferred_element_type=F32)
    lane2 = lax.broadcasted_iota(jnp.int32, (N, CAP * N), 1)
    off2 = ((lane2 >> 1) * MIX) & (N - 1)
    e2 = (((((mz + (off2 >> 5)) & 3) * 4 + ((my + ((off2 >> 3) & 3)) & 3)) * 4 + ((mx + ((off2 >> 1) & 3)) & 3)) * 2
          + ((mc + (off2 & 1)) & 1))
    expand = jnp.where(lax.broadcasted_iota(jnp.int32, (N, CAP * N), 0) == e2, 1.0, 0.0)
    lg = jnp.dot(logits, expand, precision=lax.Precision.HIGHEST, preferred_element_type=F32)
    on = snd_v[...] > 0.5
    top = jnp.max(jnp.where(on, lg, -jnp.inf), axis=-1, keepdims=True)
    ex = jnp.where(on, jnp.exp(jnp.where(on, lg - top, 0.0)), 0.0)
    gates = ex / jnp.sum(ex, axis=-1, keepdims=True)
    g1 = gates.astype(BF)
    d1 = gates - g1.astype(F32)
    g2 = d1.astype(BF)
    g3 = (d1 - g2.astype(F32)).astype(BF)
    g_v[...] = jnp.concatenate([g1, g2, g3], axis=0)
    for c in we_c:
        c.wait()

    rr = CAP * gsz
    for q in range(GRP):
        lo = 1 if q == 0 else q * gsz
        got = rbuf.at[:, pl.ds(lo, (q + 1) * gsz - lo)]
        cp(got, got, rsem.at[q]).wait()

        @pl.loop(0, FF // 256)
        def _(n):
            cols = pl.ds(pl.multiple_of(n * 256, 256), 256)
            ga = jnp.zeros((rr, 256), F32)
            ua = jnp.zeros((rr, 256), F32)
            for kk in range(8):
                xk = jnp.concatenate([rview[2 * kk, q * rr:(q + 1) * rr, :], rview[2 * kk + 1, q * rr:(q + 1) * rr, :]], axis=1)
                ga = ga + jnp.dot(xk, wg_v[kk * 256:(kk + 1) * 256, cols], preferred_element_type=F32)
                ua = ua + jnp.dot(xk, wu_v[kk * 256:(kk + 1) * 256, cols], preferred_element_type=F32)
            hid_v[q * rr:(q + 1) * rr, cols] = (jax.nn.silu(ga) * ua).astype(BF)

        @pl.loop(0, 4)
        def _(n):
            cols = pl.ds(pl.multiple_of(n * 512, 512), 512)
            o = jnp.dot(hid_v[q * rr:(q + 1) * rr, :], wd_v[:, cols], preferred_element_type=F32).astype(BF)
            for j in range(4):
                oview[n * 4 + j, q * rr:(q + 1) * rr, :] = o[:, j * 128:(j + 1) * 128]

        @pl.loop(lo, (q + 1) * gsz)
        def _(k):
            pltpu.make_async_remote_copy(obuf.at[:, k], bbuf.at[:, k], osem, bsem,
                                         device_id={"ep": shift_dev(me, offset_of(k), -1)}, device_id_type=MESH).start()
    bbuf[:, 0] = obuf[:, 0]

    got = bbuf.at[:, pl.ds(1, N - 1)]
    cp(got, got, bsem).wait()
    for n in range(4):
        back = jnp.concatenate([bview[n * 4 + j] for j in range(4)], axis=1)
        m = jnp.dot(g_v[...], back, preferred_element_type=F32)
        cols = slice(n * 512, (n + 1) * 512)
        out_ref[:, cols] = (y_v[:, cols] + (m[0:S] + m[S:2 * S] + m[2 * S:3 * S])).astype(BF)
    sent = sbuf.at[:, pl.ds(1, N - 1)]
    cp(sent, sent, ssem).wait()
    cp(sent, sent, osem).wait()
    for c in couts:
        c.wait()


def solution(mesh):
    row_spec = P(('dp', 'ep'), None)
    cache_spec = P(('dp', 'ep'), None, None, None)
    len_spec = P(('dp', 'ep'))
    rep_vec = P(None)
    rep_mat = P(None, None)
    exp_spec = P('ep', None, None)
    inv = np.power(ROPE_BASE, -np.arange(0, HD, 2).astype(np.float32) / HD).astype(np.float32)
    freq_np = np.concatenate([inv, inv])[None, :]
    dma = pltpu.SemaphoreType.DMA

    def local_step(hidden, k_cache, v_cache, seq_lens, expert_ids, ln_attn, w_q, w_k, w_v, q_gain, k_gain, w_o, ln_moe, w_router, w_gate, w_up, w_down):
        anyspec = pl.BlockSpec(memory_space=pl.ANY)
        V = pltpu.VMEM
        return pl.pallas_call(
            kernel,
            out_shape=(jax.ShapeDtypeStruct((S, D), BF),
                       jax.ShapeDtypeStruct((S, T, NKV, HD), BF), jax.ShapeDtypeStruct((S, T, NKV, HD), BF)),
            in_specs=[anyspec] * 18,
            out_specs=(pl.BlockSpec(memory_space=pltpu.VMEM), anyspec, anyspec),
            scratch_shapes=[
                V((S, D), BF), pltpu.SMEM((S,), jnp.int32), V((S, 8), jnp.int32), V((16, 128), BF), V((16, 128), BF),
                V((1, HD), BF), V((1, HD), BF), V((1, HD), F32),
                V((D, 512), BF), V((D, 512), BF), V((4, D, 1024), BF), V((4, 4096, 512), BF), V((D, N), BF),
                V((D, FF), BF), V((D, FF), BF), V((FF, D), BF),
                V((S, T, NKV, HD), BF), V((S, T, NKV, HD), BF), V((NKV, S * T, HD), BF), V((NKV, S * T, HD), BF),
                V((S, D), BF), V((2, NKV, S, HD), F32), V((S, S * T), F32), V((2, S, HD), F32), V((S, 4096), BF),
                V((S, D), F32), V((S, D), BF), V((CAP * N, S), BF), V((S, CAP * N), F32), V((3 * S, CAP * N), BF),
                V((CAP * N, FF), BF),
                V((16, N, CAP, HD), BF), V((16, N, CAP, HD), BF), V((16, N, CAP, HD), BF), V((16, N, CAP, HD), BF),
                dma((8,)), dma((2,)), dma((2,)), dma((4,)), dma((4,)), dma, dma((3,)), dma((2,)),
                dma, dma, dma((GRP,)), dma,
            ],
            compiler_params=pltpu.CompilerParams(collective_id=0, has_side_effects=True, vmem_limit_bytes=67043328),
        )(hidden, k_cache, v_cache, seq_lens, expert_ids, ln_attn.reshape(16, 128), w_q, w_k, w_v,
          q_gain.reshape(1, HD), k_gain.reshape(1, HD), w_o, ln_moe.reshape(16, 128), w_router, w_gate, w_up, w_down,
          jnp.asarray(freq_np))

    return jax.shard_map(local_step, mesh=mesh, in_specs=(row_spec, cache_spec, cache_spec, len_spec, row_spec, rep_vec, rep_mat, rep_mat, rep_mat, rep_vec, rep_vec, rep_mat, rep_vec, rep_mat, exp_spec, exp_spec, exp_spec), out_specs=(row_spec, cache_spec, cache_spec), check_vma=False)
```

time: 112 us -> 59.9 us (0.53)
  Pallas kernels: 0 us -> 52 us
  matrix products: 35 us -> 0 us
  waiting for transfers between devices: 32.7 us -> 0 us
  starting transfers between devices: 17.3 us -> 0 us
  other arithmetic: 9.49 us -> 0 us
  local copies, waits for them, and re-layouts: 16.2 us -> 6.89 us
    pallas_call x0 -> x1, Pallas kernels: none -> 52 us  [local_step(): pl.pallas_call(kernel, out_shape=(jax.ShapeDtypeStruct((S, D), BF), jax.S...]
    dot_general x10 -> x0, matrix products: 35 us -> none  [the longest x1 8.2 us: attend(): y_res = h_f32 + jnp.dot(attn_out, w_o, preferred_element_type=jnp.float32)]
    all_to_all x2 -> x0, waiting for transfers between devices: 32.7 us -> none  [the longest x1 17.4 us: local_step(): recv_rows = lax.all_to_all(send_rows, 'ep', 0, 0, tiled=True)]
    all_to_all x2 -> x0, starting transfers between devices: 17.3 us -> none  [the longest x1 12 us: local_step(): recv_rows = lax.all_to_all(send_rows, 'ep', 0, 0, tiled=True)]
    gather x9 -> x0, local copies, waits for them, and re-layouts: 6.55 us -> none  [the longest x1 3.59 us: local_step(): jnp.take(back_rows.reshape(n_experts * capacity, -1), slot_ids.reshape(-1...]
    convert_element_type x2 -> x0, local copies, waits for them, and re-layouts: 5.4 us -> none  [the longest x1 3.29 us: local_step(): jnp.einsum('secf,efd->secd', hidden_act, w_down, preferred_element_type=j...]
    unnamed x20 -> x4, local copies, waits for them, and re-layouts: 1.66 us -> 6.89 us
    reduce_sum x5 -> x0, other arithmetic: 3.18 us -> none  [the longest x1 1.96 us: local_step(): moe_out = jnp.sum(gate_vals[:, :, None] * picked, axis=1)]
  transfers between devices with their start and end apart: 2 -> 0, of which waited for: 2 -> 0; matrix products, arithmetic and copies ran while one was open for 4% -> 0% of each run, Pallas kernels for 0% -> 0%
where the time goes in v1:
time: 59.9 us; the launch traced here: 59.6 us
  Pallas kernels  52 us (87%)
  local copies, waits for them, and re-layouts  6.89 us (12%)
  between operations  0.64 us (1%)
    pallas_call x1, Pallas kernels, local_step(): pl.pallas_call(kernel, out_shape=(jax.ShapeDtypeStruct((S, D), BF), jax.S...  52 us
    unnamed x4, local copies, waits for them, and re-layouts  6.89 us

profile of v1, /device:TPU:1, one launch (start us, length us, event | category | flops | bytes accessed | tf_op | source)
XLA Modules:
  0.0 59.6 jit_solution(15502875297739744459)
XLA Ops:
  0.6 1.4 %copy.21.ids_hbm = s32[16,8]{1,0:T(8,128)} copy(s32[16,8]{0,1:T(8,128)} %param.22) | data formatting | bytes 1024 | tf_op args[4]
  2.0 52.0 %shard_map.193 = (bf16[16,2048]{1,0:T(8,128)(2,1)}, bf16[16,32,4,128]{3,2,1,0:T(4,128)(2,1)}, bf16[16,32,4,128]{3,2,1,0:T(4,128)(2,1)}) custom-call(bf16[16,2048]{1,0:T(8,128)(2,1)} %h_hbm.1, bf16[16,32,4,128]{3,2,1,0:T(4,128)(2,1)} %kc_hbm.1, bf16[16,32,4,128]{3,2,1,0:T(4,128)(2,1)} %vc_hbm.1, s32[16]{0:T(128)} %sl_hbm.1, s32[16,8]{1,0:T(8,128)} %copy.21.ids_hbm, ...), custom_call_target="tpu_custom_call" | custom-call | tf_op jit(solution)/shard_map/pallas_call | solution.py:309
  54.0 1.5 %copy.25 = bf16[16,2048]{1,0:T(8,128)(2,1)} copy(bf16[16,2048]{1,0:T(8,128)(2,1)} %get-tuple-element.6) | data formatting | bytes 131072
  55.5 2.0 %copy.26 = bf16[16,32,4,128]{3,2,1,0:T(4,128)(2,1)} copy(bf16[16,32,4,128]{3,2,1,0:T(4,128)(2,1)} %get-tuple-element.7) | data formatting | bytes 1048576
  57.5 2.0 %copy.27 = bf16[16,32,4,128]{3,2,1,0:T(4,128)(2,1)} copy(bf16[16,32,4,128]{3,2,1,0:T(4,128)(2,1)} %get-tuple-element.8) | data formatting | bytes 1048576

commit v2 on v1

v2 whole, which is shorter than its diff:
```python
import functools

import jax
import jax.numpy as jnp
import numpy as np
from jax import lax
from jax.experimental import pallas as pl
from jax.experimental.pallas import tpu as pltpu
from jax.sharding import PartitionSpec as P

MESH = pl.DeviceIdType.MESH
EPS = 1e-6
ROPE_BASE = 1000000.0
BF = jnp.bfloat16
F32 = jnp.float32
N = 128
S = 16
D = 2048
HD = 128
T = 32
NKV = 4
GQ = 8
FF = 768
CAP = 2
GRP = 2
FIN = 2


def peers(me, t, sign):
    a, b = lax.div(t, 4), lax.rem(t, 4)
    c, x, y, z = lax.rem(me, 2), lax.rem(lax.div(me, 2), 4), lax.rem(lax.div(me, 8), 4), lax.div(me, 32)
    zs = [lax.rem(z + 8 + sign * (a + f), 4) * 32 for f in range(4)]
    ys = [lax.rem(y + 8 + sign * (b + g), 4) * 8 for g in range(4)]
    xs = [lax.rem(x + 4 + sign * d, 4) * 2 for d in range(4)]
    cs = [c, 1 - c]
    return [zs[i % 4] + ys[i // 2] + (xs[i // 2] + cs[i % 2]) for i in range(8)]


def rms_rope(v, gain, cos, sin):
    ms = jnp.mean(v * v, axis=-1, keepdims=True)
    v = v * lax.rsqrt(ms + EPS) * gain
    return v * cos + pltpu.roll(v, 64, axis=1) * sin


def kernel(h_hbm, kc_hbm, vc_hbm, sl_hbm, ids_hbm, lna_hbm, wq_hbm, wk_hbm, wv_hbm, qg_hbm, kg_hbm, wo_hbm,
           lnm_hbm, wr_hbm, wg_hbm, wu_hbm, wd_hbm, freq_hbm,
           out_ref, rep_ref,
           h_v, sl_s, ids_v, lna_v, lnm_v, qg_v, kg_v, freq_v,
           wk_v, wv_v, wq_v, wo_v, wr_v, wg_v, wu_v, wd_v,
           kc_v, vc_v, kp_v, vp_v, x_v, kn_v, mask_v, trig_v, at_v, yh_v, yp_v, y_v, r_v, p_v, snd_v, g_v, hid_v,
           sbuf, rbuf, obuf, bbuf,
           sm_small, sm_kv, sm_cache, sm_wq, sm_wo, sm_wr, sm_we, as_sem, ar_sem, ys_sem, yr_sem,
           ssem, osem, rsem, bsem):
    me = lax.axis_index("ep")
    cp = pltpu.make_async_copy
    half = me % 2
    mate = me + 1 - 2 * half

    small = [cp(a, b, sm_small.at[i]) for i, (a, b) in enumerate([
        (h_hbm, h_v), (lna_hbm, lna_v), (sl_hbm, sl_s), (freq_hbm, freq_v), (kg_hbm, kg_v), (qg_hbm, qg_v),
        (ids_hbm, ids_v), (lnm_hbm, lnm_v)])]
    for c in small:
        c.start()
    kvw = [cp(wk_hbm, wk_v, sm_kv.at[0]), cp(wv_hbm, wv_v, sm_kv.at[1])]
    caches = [cp(kc_hbm, kc_v, sm_cache.at[0]), cp(vc_hbm, vc_v, sm_cache.at[1])]

    def wq_copy(g):
        return cp(wq_hbm.at[:, pl.ds(pl.multiple_of(g * 1024, 1024), 1024)], wq_v.at[g], sm_wq.at[g])

    def wo_copy(n):
        return cp(wo_hbm.at[pl.ds(n * 1024, 1024), pl.ds(pl.multiple_of(half * 1024, 1024), 1024)], wo_v.at[n], sm_wo.at[n])

    wr_c = cp(wr_hbm, wr_v, sm_wr)
    we_c = [cp(wg_hbm.at[0], wg_v, sm_we.at[0]), cp(wu_hbm.at[0], wu_v, sm_we.at[1]), cp(wd_hbm.at[0], wd_v, sm_we.at[2])]
    for c in kvw + caches:
        c.start()
    wq_copy(0).start()

    bar = pltpu.get_barrier_semaphore()

    for i in range(8):
        pl.semaphore_signal(bar, inc=1, device_id={"ep": lax.rem(me + (i + 1), N)}, device_id_type=MESH)

    @pl.loop(0, 7)
    def _(b):
        base = me + b * 17
        for i in range(17):
            pl.semaphore_signal(bar, inc=1, device_id={"ep": lax.rem(base + (i + 9), N)}, device_id_type=MESH)

    for c in small:
        c.wait()

    wq_copy(1).start()
    wq_copy(2).start()

    hf = h_v[...].astype(F32)
    rs = lax.rsqrt(jnp.mean(hf * hf, axis=-1, keepdims=True) + EPS)
    lna = lna_v[...].astype(F32)
    for j in range(16):
        sl = slice(j * 128, (j + 1) * 128)
        x_v[:, sl] = (hf[:, sl] * rs * lna[j:j + 1, :]).astype(BF)

    srow = lax.broadcasted_iota(jnp.int32, (S, 128), 0)
    lens = jnp.zeros((S, 128), jnp.int32)
    for s in range(S):
        lens = jnp.where(srow == s, sl_s[s], lens)
    ang = lens.astype(F32) * freq_v[...]
    sgn = jnp.where(lax.broadcasted_iota(jnp.int32, (S, 128), 1) < 64, -1.0, 1.0)
    cos = jnp.cos(ang)
    sin = jnp.sin(ang) * sgn
    trig_v[0] = cos
    trig_v[1] = sin
    for b in range(4):
        col = lax.broadcasted_iota(jnp.int32, (S, 128), 1) + b * 128
        ok = ((col >> 5) == srow) & ((col & 31) <= lens)
        mask_v[:, b * 128:(b + 1) * 128] = jnp.where(ok, 0.0, -1e30)

    x = x_v[...]
    kg = kg_v[...].astype(F32)
    kvw[0].wait()
    kp = jnp.dot(x, wk_v[...], preferred_element_type=F32)
    for g in range(NKV):
        kn_v[0, g] = rms_rope(kp[:, g * 128:(g + 1) * 128], kg, cos, sin)
    kvw[1].wait()
    vp = jnp.dot(x, wv_v[...], preferred_element_type=F32)
    for g in range(NKV):
        kn_v[1, g] = vp[:, g * 128:(g + 1) * 128]

    wq_copy(3).start()

    ri = lax.broadcasted_iota(jnp.int32, (256, 64), 0)
    ci = lax.broadcasted_iota(jnp.int32, (256, 64), 1)
    rep1 = jnp.where(((ri >> 4) == (ci & 15)) & ((ri & 3) == (ci >> 4)), 1.0, 0.0).astype(BF)
    pr = lax.broadcasted_iota(jnp.int32, (128, 128), 0)
    pc = lax.broadcasted_iota(jnp.int32, (128, 128), 1)
    perm = jnp.where(((pr & 31) == (pc >> 2)) & ((pr >> 5) == (pc & 3)), 1.0, 0.0).astype(BF)
    trow = pr >> 2
    for i, (buf, dst) in enumerate(((kc_v, kp_v), (vc_v, vp_v))):
        caches[i].wait()
        rows = buf.reshape(S * T * NKV, HD)
        new = jnp.concatenate([kn_v[i, g].astype(BF) for g in range(NKV)], axis=0)
        rep = jnp.dot(rep1, new, preferred_element_type=F32)
        rep_ref[i] = rep.astype(BF)
        for s in range(S):
            old = rows[s * 128:(s + 1) * 128, :].astype(F32)
            rep_s = jnp.concatenate([rep[s * 16:(s + 1) * 16, :]] * 8, axis=0)
            upd = jnp.where(trow == sl_s[s], rep_s, old).astype(BF)
            grp = jnp.dot(perm, upd, preferred_element_type=F32).astype(BF)
            for g in range(NKV):
                dst[g, s * 32:(s + 1) * 32, :] = grp[g * 32:(g + 1) * 32, :]

    def at_copy(g):
        return pltpu.make_async_remote_copy(at_v.at[g, pl.ds(0, S)], at_v.at[g, pl.ds(S, S)], as_sem.at[g], ar_sem.at[g],
                                            device_id={"ep": mate}, device_id_type=MESH)
    pl.semaphore_wait(bar, N - 1)

    qg = qg_v[...].astype(F32)

    def attend(g, q):
        sc = lax.dot_general(q, kp_v[g], (((1,), (1,)), ((), ())), preferred_element_type=F32)
        mk = mask_v[...]
        sc = jnp.where(jnp.concatenate([mk] * GQ, axis=0) == 0.0, sc * (HD ** -0.5), -1e30)
        ex = jnp.exp(sc - jnp.max(sc, axis=-1, keepdims=True))
        pb = (ex / jnp.sum(ex, axis=-1, keepdims=True)).astype(BF)
        o = jnp.dot(pb, vp_v[g], preferred_element_type=F32).astype(BF)
        for j in range(GQ):
            at_v[g, 0:S, j * 128:(j + 1) * 128] = o[j * S:(j + 1) * S, :]

    prev = None
    for g in range(NKV):
        wq_copy(g).wait()
        if g == 0:
            wo_copy(0).start()
            wo_copy(1).start()
        elif g < 3:
            wo_copy(g + 1).start()
        else:
            wr_c.start()
            we_c[0].start()
        q = jnp.dot(x_v[...], wq_v[g], preferred_element_type=F32)
        if g:
            attend(g - 1, prev)
        q = jnp.concatenate([q[:, j * 128:(j + 1) * 128] for j in range(GQ)], axis=0)
        cs = jnp.concatenate([trig_v[0]] * GQ, axis=0)
        sn = jnp.concatenate([trig_v[1]] * GQ, axis=0)
        prev = rms_rope(q, qg, cs, sn).astype(BF)
        if g:
            at_copy(g - 1).start()
    attend(3, prev)
    at_copy(3).start()

    yn = None
    for g in range(NKV):
        wo_copy(g).wait()
        at_copy(g).wait()
        if g < 2:
            we_c[g + 1].start()
        part = jnp.dot(at_v[g], wo_v[g], preferred_element_type=F32)
        yn = part if g == 0 else yn + part
    yh_v[half] = yn[0:S]
    yp_v[...] = yn[S:2 * S]
    ycp = pltpu.make_async_remote_copy(yp_v, yh_v.at[half], ys_sem, yr_sem, device_id={"ep": mate}, device_id_type=MESH)
    ycp.start()

    mc, mx, my, mz = me % 2, me // 2 % 4, me // 8 % 4, me // 32

    def expert_at(slot):
        i, b, a = (slot >> 1) & 7, (slot >> 4) & 3, slot >> 6
        return (((((mz + a + i) & 3) * 4 + ((my + b + (i >> 1)) & 3)) * 4 + ((mx + (i >> 1)) & 3)) * 2 + ((mc + i) & 1))
    slot = lax.broadcasted_iota(jnp.int32, (CAP * N, S), 0)
    e_col = expert_at(slot)
    ids = ids_v[...]
    chosen = jnp.zeros((CAP * N, S), F32)
    for k in range(8):
        chosen = chosen + jnp.where(ids[k:k + 1, :] == e_col, 1.0, 0.0)
    tri = jnp.where(lax.broadcasted_iota(jnp.int32, (S, S), 0) < lax.broadcasted_iota(jnp.int32, (S, S), 1), 1.0, 0.0)
    rank = jnp.dot(chosen.astype(BF), tri.astype(BF), preferred_element_type=F32)
    send = chosen * jnp.where(rank == (slot & 1).astype(F32), 1.0, 0.0)
    snd_v[...] = jnp.transpose(send)
    p_v[...] = send.astype(BF)

    ycp.wait()
    y = h_v[...].astype(F32) + jnp.concatenate([yh_v[0], yh_v[1]], axis=1)
    y_v[...] = y
    rs = lax.rsqrt(jnp.mean(y * y, axis=-1, keepdims=True) + EPS)
    lnm = lnm_v[...].astype(F32)
    for j in range(16):
        sl = slice(j * 128, (j + 1) * 128)
        r_v[:, sl] = (y[:, sl] * rs * lnm[j:j + 1, :]).astype(BF)

    sview, rview = sbuf.reshape(16, CAP * N, HD), rbuf.reshape(16, CAP * N, HD)
    oview, bview = obuf.reshape(16, CAP * N, HD), bbuf.reshape(16, CAP * N, HD)
    for n in range(4):
        rows = jnp.dot(p_v[...], r_v[:, n * 512:(n + 1) * 512], preferred_element_type=F32).astype(BF)
        for j in range(4):
            sview[n * 4 + j] = rows[:, j * 128:(j + 1) * 128]
    gsz = N // GRP

    def push(src, dst, s_sem, r_sem, t, sign):
        for i, to in enumerate(peers(me, t, sign)):
            if not (isinstance(t, int) and t * 8 + i == 0):
                k = t * 8 + i
                pltpu.make_async_remote_copy(src.at[:, k], dst.at[:, k], s_sem, r_sem, device_id={"ep": to}, device_id_type=MESH).start()

    def push_group(src, dst, s_sem, r_sem, q, sign):
        if q == 0:
            push(src, dst, s_sem, r_sem, 0, sign)

        @pl.loop(max(1, q * gsz // 8), (q + 1) * gsz // 8)
        def _(t):
            push(src, dst, s_sem, r_sem, t, sign)
    for q in range(GRP):
        push_group(sbuf, rbuf, ssem, rsem.at[q], q, 1)
    rbuf[:, 0] = sbuf[:, 0]

    wr_c.wait()
    logits = jnp.dot(r_v[...], wr_v[...], preferred_element_type=F32)
    e2 = expert_at(lax.broadcasted_iota(jnp.int32, (N, CAP * N), 1))
    expand = jnp.where(lax.broadcasted_iota(jnp.int32, (N, CAP * N), 0) == e2, 1.0, 0.0)
    lg = jnp.dot(logits, expand, precision=lax.Precision.HIGHEST, preferred_element_type=F32)
    on = snd_v[...] > 0.5
    top = jnp.max(jnp.where(on, lg, -jnp.inf), axis=-1, keepdims=True)
    ex = jnp.where(on, jnp.exp(jnp.where(on, lg - top, 0.0)), 0.0)
    gates = ex / jnp.sum(ex, axis=-1, keepdims=True)
    g1 = gates.astype(BF)
    d1 = gates - g1.astype(F32)
    g2 = d1.astype(BF)
    g3 = (d1 - g2.astype(F32)).astype(BF)
    g_v[...] = jnp.concatenate([g1, g2, g3], axis=0)
    for c in we_c:
        c.wait()

    rr = CAP * gsz
    for q in range(GRP):
        lo = 1 if q == 0 else q * gsz
        got = rbuf.at[:, pl.ds(lo, (q + 1) * gsz - lo)]
        cp(got, got, rsem.at[q]).wait()

        for n in range(FF // 256):
            cols = slice(n * 256, (n + 1) * 256)
            ga = jnp.zeros((rr, 256), F32)
            ua = jnp.zeros((rr, 256), F32)
            for kk in range(8):
                xk = jnp.concatenate([rview[2 * kk, q * rr:(q + 1) * rr, :], rview[2 * kk + 1, q * rr:(q + 1) * rr, :]], axis=1)
                ga = ga + jnp.dot(xk, wg_v[kk * 256:(kk + 1) * 256, cols], preferred_element_type=F32)
                ua = ua + jnp.dot(xk, wu_v[kk * 256:(kk + 1) * 256, cols], preferred_element_type=F32)
            hid_v[q * rr:(q + 1) * rr, cols] = (jax.nn.silu(ga) * ua).astype(BF)

        for n in range(4):
            cols = slice(n * 512, (n + 1) * 512)
            o = jnp.dot(hid_v[q * rr:(q + 1) * rr, :], wd_v[:, cols], preferred_element_type=F32).astype(BF)
            for j in range(4):
                oview[n * 4 + j, q * rr:(q + 1) * rr, :] = o[:, j * 128:(j + 1) * 128]

        push_group(obuf, bbuf, osem, bsem, q, -1)
    bbuf[:, 0] = obuf[:, 0]

    got = bbuf.at[:, pl.ds(1, N - 1)]
    cp(got, got, bsem).wait()
    for n in range(4):
        back = jnp.concatenate([bview[n * 4 + j] for j in range(4)], axis=1)
        m = jnp.dot(g_v[...], back, preferred_element_type=F32)
        cols = slice(n * 512, (n + 1) * 512)
        out_ref[:, cols] = (y_v[:, cols] + (m[0:S] + m[S:2 * S] + m[2 * S:3 * S])).astype(BF)
    sent = sbuf.at[:, pl.ds(1, N - 1)]
    cp(sent, sent, ssem).wait()
    cp(sent, sent, osem).wait()


def finish(out_hbm, fresh_hbm, kc_hbm, vc_hbm, sl_hbm, res_hbm, ko_hbm, vo_hbm, out_v, fresh_v, c_v, sl_s, sm_in, sm_c, sm_res, sm_o):
    cp = pltpu.make_async_copy
    step = S // FIN
    ins = [cp(sl_hbm, sl_s, sm_in.at[0]), cp(fresh_hbm, fresh_v, sm_in.at[1]), cp(out_hbm, out_v, sm_in.at[2])]
    parts = [(i, p) for p in range(FIN) for i in range(2)]
    cin = {(i, p): cp((kc_hbm, vc_hbm)[i].at[pl.ds(p * step, step)], c_v.at[i, pl.ds(p * step, step)], sm_c.at[i, p]) for i, p in parts}
    cout = {(i, p): cp(c_v.at[i, pl.ds(p * step, step)], (ko_hbm, vo_hbm)[i].at[pl.ds(p * step, step)], sm_o.at[i, p]) for i, p in parts}
    for c in ins:
        c.start()
    for key in parts:
        cin[key].start()
    ins[2].wait()
    res = cp(out_v, res_hbm, sm_res)
    res.start()
    ins[0].wait()
    ins[1].wait()
    trow = lax.broadcasted_iota(jnp.int32, (128, HD), 0) >> 2
    rows = c_v.reshape(2, S * T * NKV, HD)
    for i, p in parts:
        cin[i, p].wait()
        for s in range(p * step, (p + 1) * step):
            old = rows[i, s * 128:(s + 1) * 128, :].astype(F32)
            new = jnp.concatenate([fresh_v[i, s * 16:(s + 1) * 16, :].astype(F32)] * 8, axis=0)
            rows[i, s * 128:(s + 1) * 128, :] = jnp.where(trow == sl_s[s], new, old).astype(BF)
        cout[i, p].start()
    res.wait()
    for key in parts:
        cout[key].wait()


def solution(mesh):
    row_spec = P(('dp', 'ep'), None)
    cache_spec = P(('dp', 'ep'), None, None, None)
    len_spec = P(('dp', 'ep'))
    rep_vec = P(None)
    rep_mat = P(None, None)
    exp_spec = P('ep', None, None)
    inv = np.power(ROPE_BASE, -np.arange(0, HD, 2).astype(np.float32) / HD).astype(np.float32)
    freq_np = np.concatenate([inv, inv])[None, :]
    dma = pltpu.SemaphoreType.DMA

    def local_step(hidden, k_cache, v_cache, seq_lens, expert_ids, ln_attn, w_q, w_k, w_v, q_gain, k_gain, w_o, ln_moe, w_router, w_gate, w_up, w_down):
        anyspec = pl.BlockSpec(memory_space=pl.ANY)
        V = pltpu.VMEM
        out, fresh = pl.pallas_call(
            kernel,
            out_shape=(jax.ShapeDtypeStruct((S, D), BF), jax.ShapeDtypeStruct((2, 256, HD), BF)),
            in_specs=[anyspec] * 18,
            out_specs=(pl.BlockSpec(memory_space=pltpu.VMEM),) * 2,
            scratch_shapes=[
                V((S, D), BF), pltpu.SMEM((S,), jnp.int32), V((8, S), jnp.int32), V((16, 128), BF), V((16, 128), BF),
                V((1, HD), BF), V((1, HD), BF), V((1, HD), F32),
                V((D, 512), BF), V((D, 512), BF), V((4, D, 1024), BF), V((4, 1024, 1024), BF), V((D, N), BF),
                V((D, FF), BF), V((D, FF), BF), V((FF, D), BF),
                V((S, T, NKV, HD), BF), V((S, T, NKV, HD), BF), V((NKV, S * T, HD), BF), V((NKV, S * T, HD), BF),
                V((S, D), BF), V((2, NKV, S, HD), F32), V((S, S * T), F32), V((2, S, HD), F32), V((NKV, 2 * S, 1024), BF), V((2, S, 1024), F32), V((S, 1024), F32),
                V((S, D), F32), V((S, D), BF), V((CAP * N, S), BF), V((S, CAP * N), F32), V((3 * S, CAP * N), BF),
                V((CAP * N, FF), BF),
                V((16, N, CAP, HD), BF), V((16, N, CAP, HD), BF), V((16, N, CAP, HD), BF), V((16, N, CAP, HD), BF),
                dma((8,)), dma((2,)), dma((2,)), dma((4,)), dma((4,)), dma, dma((3,)), dma((4,)), dma((4,)), dma, dma,
                dma, dma, dma((GRP,)), dma,
            ],
            compiler_params=pltpu.CompilerParams(collective_id=0, has_side_effects=True, vmem_limit_bytes=67043328),
        )(hidden, k_cache, v_cache, seq_lens, expert_ids.T, ln_attn.reshape(16, 128), w_q, w_k, w_v,
          q_gain.reshape(1, HD), k_gain.reshape(1, HD), w_o, ln_moe.reshape(16, 128), w_router, w_gate, w_up, w_down,
          jnp.asarray(freq_np))
        return pl.pallas_call(
            finish,
            out_shape=(jax.ShapeDtypeStruct((S, D), BF),
                       jax.ShapeDtypeStruct((S, T, NKV, HD), BF), jax.ShapeDtypeStruct((S, T, NKV, HD), BF)),
            in_specs=[anyspec] * 5,
            out_specs=(anyspec,) * 3,
            scratch_shapes=[V((S, D), BF), V((2, 256, HD), BF), V((2, S, T, NKV, HD), BF), pltpu.SMEM((S,), jnp.int32),
                            dma((3,)), dma((2, FIN)), dma, dma((2, FIN))],
        )(out, fresh, k_cache, v_cache, seq_lens)

    return jax.shard_map(local_step, mesh=mesh, in_specs=(row_spec, cache_spec, cache_spec, len_spec, row_spec, rep_vec, rep_mat, rep_mat, rep_mat, rep_vec, rep_vec, rep_mat, rep_vec, rep_mat, exp_spec, exp_spec, exp_spec), out_specs=(row_spec, cache_spec, cache_spec), check_vma=False)
```

time: 59.9 us -> 52.5 us (0.88)
  local copies, waits for them, and re-layouts: 6.89 us -> 0 us
    unnamed x4 -> x0, local copies, waits for them, and re-layouts: 6.89 us -> none
    pallas_call x1, Pallas kernels: 52 us -> 49 us  [local_step(): pl.pallas_call(kernel, out_shape=(jax.ShapeDtypeStruct((S, D), BF), jax.S...]
    pallas_call x0 -> x1, Pallas kernels: none -> 2.57 us  [local_step(): pl.pallas_call(finish, out_shape=(jax.ShapeDtypeStruct((S, D), BF), jax.S...]
where the time goes in v2:
time: 52.5 us; the launch traced here: 52.2 us
  Pallas kernels  51.6 us (98%)
  between operations  0.64 us (1%)
    pallas_call x1, Pallas kernels, local_step(): pl.pallas_call(kernel, out_shape=(jax.ShapeDtypeStruct((S, D), BF), jax.S...  49 us
    pallas_call x1, Pallas kernels, local_step(): pl.pallas_call(finish, out_shape=(jax.ShapeDtypeStruct((S, D), BF), jax.S...  2.57 us

profile of v2, /device:TPU:1, one launch (start us, length us, event | category | flops | bytes accessed | tf_op | source)
XLA Modules:
  0.0 52.2 jit_solution(1208375736691080349)
XLA Ops:
  0.6 49.0 %shard_map.193 = (bf16[16,2048]{1,0:T(8,128)(2,1)}, bf16[2,256,128]{2,1,0:T(8,128)(2,1)}) custom-call(bf16[16,2048]{1,0:T(8,128)(2,1)} %h_hbm.1, bf16[16,32,4,128]{3,2,1,0:T(4,128)(2,1)} %kc_hbm.3, bf16[16,32,4,128]{3,2,1,0:T(4,128)(2,1)} %vc_hbm.3, s32[16]{0:T(128)} %sl_hbm.3, s32[8,16]{1,0:T(8,128)} %bitcast.5, bf16[16,128]{1,0:T(8,128)(2,1)} %bitcast.6, ...), custom_call_target="tpu_custom_call" | custom-call | tf_op jit(solution)/shard_map/pallas_call | solution.py:354
  49.7 2.6 %shard_map.194 = (bf16[16,2048]{1,0:T(8,128)(2,1)}, bf16[16,32,4,128]{3,2,1,0:T(4,128)(2,1)}, bf16[16,32,4,128]{3,2,1,0:T(4,128)(2,1)}) custom-call(bf16[16,2048]{1,0:T(8,128)(2,1)} %get-tuple-element.5.out_hbm, bf16[2,256,128]{2,1,0:T(8,128)(2,1)} %get-tuple-element.6.fresh_hbm, bf16[16,32,4,128]{3,2,1,0:T(4,128)(2,1)} %kc_hbm.3, ...), custom_call_target="tpu_custom_call" | custom-call | tf_op jit(solution)/shard_map/pallas_call | solution.py:376

commit v3 on v2

--- a/solution.py
+++ b/solution.py
@@ -22,18 +22,21 @@
 GQ = 8
 FF = 768
 CAP = 2
-GRP = 2
-FIN = 2
+GROUPS = ((0, 8), (8, 16))
+GRP = len(GROUPS)
+MUL = 91
+STEP = 11
 
 
 def peers(me, t, sign):
-    a, b = lax.div(t, 4), lax.rem(t, 4)
     c, x, y, z = lax.rem(me, 2), lax.rem(lax.div(me, 2), 4), lax.rem(lax.div(me, 8), 4), lax.div(me, 32)
+    u = lax.rem(t * STEP, 16)
+    a, b = lax.div(u, 4), lax.rem(u, 4)
     zs = [lax.rem(z + 8 + sign * (a + f), 4) * 32 for f in range(4)]
     ys = [lax.rem(y + 8 + sign * (b + g), 4) * 8 for g in range(4)]
-    xs = [lax.rem(x + 4 + sign * d, 4) * 2 for d in range(4)]
-    cs = [c, 1 - c]
-    return [zs[i % 4] + ys[i // 2] + (xs[i // 2] + cs[i % 2]) for i in range(8)]
+    xs = [[lax.rem(x + 4 + sign * d, 4) * 2 + e for e in (c, 1 - c)] for d in range(4)]
+    offs = [i * MUL % N for i in range(8)]
+    return [zs[o // 32] + ys[o // 8 % 4] + xs[o // 2 % 4][o % 2] for o in offs]
 
 
 def rms_rope(v, gain, cos, sin):
@@ -44,10 +47,10 @@
 
 def kernel(h_hbm, kc_hbm, vc_hbm, sl_hbm, ids_hbm, lna_hbm, wq_hbm, wk_hbm, wv_hbm, qg_hbm, kg_hbm, wo_hbm,
            lnm_hbm, wr_hbm, wg_hbm, wu_hbm, wd_hbm, freq_hbm,
-           out_ref, rep_ref,
+           out_ref, kc_v, vc_v,
            h_v, sl_s, ids_v, lna_v, lnm_v, qg_v, kg_v, freq_v,
            wk_v, wv_v, wq_v, wo_v, wr_v, wg_v, wu_v, wd_v,
-           kc_v, vc_v, kp_v, vp_v, x_v, kn_v, mask_v, trig_v, at_v, yh_v, yp_v, y_v, r_v, p_v, snd_v, g_v, hid_v,
+           kp_v, vp_v, x_v, kn_v, mask_v, trig_v, at_v, yh_v, yp_v, y_v, r_v, p_v, snd_v, g_v, hid_v,
            sbuf, rbuf, obuf, bbuf,
            sm_small, sm_kv, sm_cache, sm_wq, sm_wo, sm_wr, sm_we, as_sem, ar_sem, ys_sem, yr_sem,
            ssem, osem, rsem, bsem):
@@ -140,11 +143,11 @@
         rows = buf.reshape(S * T * NKV, HD)
         new = jnp.concatenate([kn_v[i, g].astype(BF) for g in range(NKV)], axis=0)
         rep = jnp.dot(rep1, new, preferred_element_type=F32)
-        rep_ref[i] = rep.astype(BF)
         for s in range(S):
             old = rows[s * 128:(s + 1) * 128, :].astype(F32)
             rep_s = jnp.concatenate([rep[s * 16:(s + 1) * 16, :]] * 8, axis=0)
             upd = jnp.where(trow == sl_s[s], rep_s, old).astype(BF)
+            rows[s * 128:(s + 1) * 128, :] = upd
             grp = jnp.dot(perm, upd, preferred_element_type=F32).astype(BF)
             for g in range(NKV):
                 dst[g, s * 32:(s + 1) * 32, :] = grp[g * 32:(g + 1) * 32, :]
@@ -152,7 +155,6 @@
     def at_copy(g):
         return pltpu.make_async_remote_copy(at_v.at[g, pl.ds(0, S)], at_v.at[g, pl.ds(S, S)], as_sem.at[g], ar_sem.at[g],
                                             device_id={"ep": mate}, device_id_type=MESH)
-    pl.semaphore_wait(bar, N - 1)
 
     qg = qg_v[...].astype(F32)
 
@@ -184,6 +186,8 @@
         cs = jnp.concatenate([trig_v[0]] * GQ, axis=0)
         sn = jnp.concatenate([trig_v[1]] * GQ, axis=0)
         prev = rms_rope(q, qg, cs, sn).astype(BF)
+        if g == 1:
+            pl.semaphore_wait(bar, N - 1)
         if g:
             at_copy(g - 1).start()
     attend(3, prev)
@@ -205,8 +209,9 @@
     mc, mx, my, mz = me % 2, me // 2 % 4, me // 8 % 4, me // 32
 
     def expert_at(slot):
-        i, b, a = (slot >> 1) & 7, (slot >> 4) & 3, slot >> 6
-        return (((((mz + a + i) & 3) * 4 + ((my + b + (i >> 1)) & 3)) * 4 + ((mx + (i >> 1)) & 3)) * 2 + ((mc + i) & 1))
+        o, u = (((slot >> 1) & 7) * MUL) & (N - 1), (slot >> 4) * STEP
+        return (((((mz + (u >> 2) + (o >> 5)) & 3) * 4 + ((my + u + (o >> 3)) & 3)) * 4 + ((mx + (o >> 1)) & 3)) * 2
+                + ((mc + o) & 1))
     slot = lax.broadcasted_iota(jnp.int32, (CAP * N, S), 0)
     e_col = expert_at(slot)
     ids = ids_v[...]
@@ -230,11 +235,6 @@
 
     sview, rview = sbuf.reshape(16, CAP * N, HD), rbuf.reshape(16, CAP * N, HD)
     oview, bview = obuf.reshape(16, CAP * N, HD), bbuf.reshape(16, CAP * N, HD)
-    for n in range(4):
-        rows = jnp.dot(p_v[...], r_v[:, n * 512:(n + 1) * 512], preferred_element_type=F32).astype(BF)
-        for j in range(4):
-            sview[n * 4 + j] = rows[:, j * 128:(j + 1) * 128]
-    gsz = N // GRP
 
     def push(src, dst, s_sem, r_sem, t, sign):
         for i, to in enumerate(peers(me, t, sign)):
@@ -243,13 +243,18 @@
                 pltpu.make_async_remote_copy(src.at[:, k], dst.at[:, k], s_sem, r_sem, device_id={"ep": to}, device_id_type=MESH).start()
 
     def push_group(src, dst, s_sem, r_sem, q, sign):
-        if q == 0:
+        if GROUPS[q][0] == 0:
             push(src, dst, s_sem, r_sem, 0, sign)
 
-        @pl.loop(max(1, q * gsz // 8), (q + 1) * gsz // 8)
+        @pl.loop(max(1, GROUPS[q][0]), GROUPS[q][1])
         def _(t):
             push(src, dst, s_sem, r_sem, t, sign)
     for q in range(GRP):
+        r0, r1 = GROUPS[q][0] * 8 * CAP, GROUPS[q][1] * 8 * CAP
+        for n in range(4):
+            rows = jnp.dot(p_v[r0:r1, :], r_v[:, n * 512:(n + 1) * 512], preferred_element_type=F32).astype(BF)
+            for j in range(4):
+                sview[n * 4 + j, r0:r1, :] = rows[:, j * 128:(j + 1) * 128]
         push_group(sbuf, rbuf, ssem, rsem.at[q], q, 1)
     rbuf[:, 0] = sbuf[:, 0]
 
@@ -270,27 +275,27 @@
     for c in we_c:
         c.wait()
 
-    rr = CAP * gsz
     for q in range(GRP):
-        lo = 1 if q == 0 else q * gsz
-        got = rbuf.at[:, pl.ds(lo, (q + 1) * gsz - lo)]
+        lo, hi = max(1, GROUPS[q][0] * 8), GROUPS[q][1] * 8
+        r0, r1 = GROUPS[q][0] * 8 * CAP, hi * CAP
+        got = rbuf.at[:, pl.ds(lo, hi - lo)]
         cp(got, got, rsem.at[q]).wait()
 
         for n in range(FF // 256):
             cols = slice(n * 256, (n + 1) * 256)
-            ga = jnp.zeros((rr, 256), F32)
-            ua = jnp.zeros((rr, 256), F32)
+            ga = jnp.zeros((r1 - r0, 256), F32)
+            ua = jnp.zeros((r1 - r0, 256), F32)
             for kk in range(8):
-                xk = jnp.concatenate([rview[2 * kk, q * rr:(q + 1) * rr, :], rview[2 * kk + 1, q * rr:(q + 1) * rr, :]], axis=1)
+                xk = jnp.concatenate([rview[2 * kk, r0:r1, :], rview[2 * kk + 1, r0:r1, :]], axis=1)
                 ga = ga + jnp.dot(xk, wg_v[kk * 256:(kk + 1) * 256, cols], preferred_element_type=F32)
                 ua = ua + jnp.dot(xk, wu_v[kk * 256:(kk + 1) * 256, cols], preferred_element_type=F32)
-            hid_v[q * rr:(q + 1) * rr, cols] = (jax.nn.silu(ga) * ua).astype(BF)
+            hid_v[r0:r1, cols] = (jax.nn.silu(ga) * ua).astype(BF)
 
         for n in range(4):
             cols = slice(n * 512, (n + 1) * 512)
-            o = jnp.dot(hid_v[q * rr:(q + 1) * rr, :], wd_v[:, cols], preferred_element_type=F32).astype(BF)
+            o = jnp.dot(hid_v[r0:r1, :], wd_v[:, cols], preferred_element_type=F32).astype(BF)
             for j in range(4):
-                oview[n * 4 + j, q * rr:(q + 1) * rr, :] = o[:, j * 128:(j + 1) * 128]
+                oview[n * 4 + j, r0:r1, :] = o[:, j * 128:(j + 1) * 128]
 
         push_group(obuf, bbuf, osem, bsem, q, -1)
     bbuf[:, 0] = obuf[:, 0]
@@ -307,34 +312,12 @@
     cp(sent, sent, osem).wait()
 
 
-def finish(out_hbm, fresh_hbm, kc_hbm, vc_hbm, sl_hbm, res_hbm, ko_hbm, vo_hbm, out_v, fresh_v, c_v, sl_s, sm_in, sm_c, sm_res, sm_o):
-    cp = pltpu.make_async_copy
-    step = S // FIN
-    ins = [cp(sl_hbm, sl_s, sm_in.at[0]), cp(fresh_hbm, fresh_v, sm_in.at[1]), cp(out_hbm, out_v, sm_in.at[2])]
-    parts = [(i, p) for p in range(FIN) for i in range(2)]
-    cin = {(i, p): cp((kc_hbm, vc_hbm)[i].at[pl.ds(p * step, step)], c_v.at[i, pl.ds(p * step, step)], sm_c.at[i, p]) for i, p in parts}
-    cout = {(i, p): cp(c_v.at[i, pl.ds(p * step, step)], (ko_hbm, vo_hbm)[i].at[pl.ds(p * step, step)], sm_o.at[i, p]) for i, p in parts}
-    for c in ins:
+def finish(a_ref, b_ref, c_ref, a_out, b_out, c_out, sems):
+    copies = [pltpu.make_async_copy(x, y, sems.at[i]) for i, (x, y) in enumerate(((a_ref, a_out), (b_ref, b_out), (c_ref, c_out)))]
+    for c in copies:
         c.start()
-    for key in parts:
-        cin[key].start()
-    ins[2].wait()
-    res = cp(out_v, res_hbm, sm_res)
-    res.start()
-    ins[0].wait()
-    ins[1].wait()
-    trow = lax.broadcasted_iota(jnp.int32, (128, HD), 0) >> 2
-    rows = c_v.reshape(2, S * T * NKV, HD)
-    for i, p in parts:
-        cin[i, p].wait()
-        for s in range(p * step, (p + 1) * step):
-            old = rows[i, s * 128:(s + 1) * 128, :].astype(F32)
-            new = jnp.concatenate([fresh_v[i, s * 16:(s + 1) * 16, :].astype(F32)] * 8, axis=0)
-            rows[i, s * 128:(s + 1) * 128, :] = jnp.where(trow == sl_s[s], new, old).astype(BF)
-        cout[i, p].start()
-    res.wait()
-    for key in parts:
-        cout[key].wait()
+    for c in copies:
+        c.wait()
 
 
 def solution(mesh):
@@ -351,17 +334,17 @@
     def local_step(hidden, k_cache, v_cache, seq_lens, expert_ids, ln_attn, w_q, w_k, w_v, q_gain, k_gain, w_o, ln_moe, w_router, w_gate, w_up, w_down):
         anyspec = pl.BlockSpec(memory_space=pl.ANY)
         V = pltpu.VMEM
-        out, fresh = pl.pallas_call(
+        made = pl.pallas_call(
             kernel,
-            out_shape=(jax.ShapeDtypeStruct((S, D), BF), jax.ShapeDtypeStruct((2, 256, HD), BF)),
+            out_shape=(V((S, D), BF), V((S, T, NKV, HD), BF), V((S, T, NKV, HD), BF)),
             in_specs=[anyspec] * 18,
-            out_specs=(pl.BlockSpec(memory_space=pltpu.VMEM),) * 2,
+            out_specs=(pl.BlockSpec(memory_space=pltpu.VMEM),) * 3,
             scratch_shapes=[
                 V((S, D), BF), pltpu.SMEM((S,), jnp.int32), V((8, S), jnp.int32), V((16, 128), BF), V((16, 128), BF),
                 V((1, HD), BF), V((1, HD), BF), V((1, HD), F32),
                 V((D, 512), BF), V((D, 512), BF), V((4, D, 1024), BF), V((4, 1024, 1024), BF), V((D, N), BF),
                 V((D, FF), BF), V((D, FF), BF), V((FF, D), BF),
-                V((S, T, NKV, HD), BF), V((S, T, NKV, HD), BF), V((NKV, S * T, HD), BF), V((NKV, S * T, HD), BF),
+                V((NKV, S * T, HD), BF), V((NKV, S * T, HD), BF),
                 V((S, D), BF), V((2, NKV, S, HD), F32), V((S, S * T), F32), V((2, S, HD), F32), V((NKV, 2 * S, 1024), BF), V((2, S, 1024), F32), V((S, 1024), F32),
                 V((S, D), F32), V((S, D), BF), V((CAP * N, S), BF), V((S, CAP * N), F32), V((3 * S, CAP * N), BF),
                 V((CAP * N, FF), BF),
@@ -369,7 +352,7 @@
                 dma((8,)), dma((2,)), dma((2,)), dma((4,)), dma((4,)), dma, dma((3,)), dma((4,)), dma((4,)), dma, dma,
                 dma, dma, dma((GRP,)), dma,
             ],
-            compiler_params=pltpu.CompilerParams(collective_id=0, has_side_effects=True, vmem_limit_bytes=67043328),
+            compiler_params=pltpu.CompilerParams(collective_id=0, has_side_effects=True, vmem_limit_bytes=60 * 1024 * 1024),
         )(hidden, k_cache, v_cache, seq_lens, expert_ids.T, ln_attn.reshape(16, 128), w_q, w_k, w_v,
           q_gain.reshape(1, HD), k_gain.reshape(1, HD), w_o, ln_moe.reshape(16, 128), w_router, w_gate, w_up, w_down,
           jnp.asarray(freq_np))
@@ -377,10 +360,9 @@
             finish,
             out_shape=(jax.ShapeDtypeStruct((S, D), BF),
                        jax.ShapeDtypeStruct((S, T, NKV, HD), BF), jax.ShapeDtypeStruct((S, T, NKV, HD), BF)),
-            in_specs=[anyspec] * 5,
+            in_specs=[pl.BlockSpec(memory_space=pltpu.VMEM)] * 3,
             out_specs=(anyspec,) * 3,
-            scratch_shapes=[V((S, D), BF), V((2, 256, HD), BF), V((2, S, T, NKV, HD), BF), pltpu.SMEM((S,), jnp.int32),
-                            dma((3,)), dma((2, FIN)), dma, dma((2, FIN))],
-        )(out, fresh, k_cache, v_cache, seq_lens)
+            scratch_shapes=[dma((3,))],
+        )(*[pltpu.with_memory_space_constraint(m, pltpu.VMEM) for m in made])
 
     return jax.shard_map(local_step, mesh=mesh, in_specs=(row_spec, cache_spec, cache_spec, len_spec, row_spec, rep_vec, rep_mat, rep_mat, rep_mat, rep_vec, rep_vec, rep_mat, rep_vec, rep_mat, exp_spec, exp_spec, exp_spec), out_specs=(row_spec, cache_spec, cache_spec), check_vma=False)

time: 52.5 us -> 47.6 us (0.907)
  Pallas kernels: 51.6 us -> 46.8 us
    pallas_call x1, Pallas kernels: 49 us -> 45.8 us  [local_step(): pl.pallas_call(kernel, out_shape=(V((S, D), BF), V((S, T, NKV, HD), BF),...]
    pallas_call x1, Pallas kernels: 2.57 us -> 1.02 us  [local_step(): pl.pallas_call(finish, out_shape=(jax.ShapeDtypeStruct((S, D), BF), jax.S...]
where the time goes in v3:
time: 47.6 us; the launch traced here: 47.4 us
  Pallas kernels  46.8 us (98%)
  between operations  0.65 us (1%)
    pallas_call x1, Pallas kernels, local_step(): pl.pallas_call(kernel, out_shape=(V((S, D), BF), V((S, T, NKV, HD), BF),...  45.8 us
    pallas_call x1, Pallas kernels, local_step(): pl.pallas_call(finish, out_shape=(jax.ShapeDtypeStruct((S, D), BF), jax.S...  1.02 us

profile of v3, /device:TPU:1, one launch (start us, length us, event | category | flops | bytes accessed | tf_op | source)
XLA Modules:
  0.0 47.4 jit_solution(4795168448725820523)
XLA Ops:
  0.6 45.8 %shard_map.193 = (bf16[16,2048]{1,0:T(8,128)(2,1)S(1)}, bf16[16,32,4,128]{3,2,1,0:T(4,128)(2,1)S(1)}, bf16[16,32,4,128]{3,2,1,0:T(4,128)(2,1)S(1)}) custom-call(bf16[16,2048]{1,0:T(8,128)(2,1)} %h_hbm.1, bf16[16,32,4,128]{3,2,1,0:T(4,128)(2,1)} %kc_hbm.1, bf16[16,32,4,128]{3,2,1,0:T(4,128)(2,1)} %vc_hbm.1, s32[16]{0:T(128)} %sl_hbm.1, s32[8,16]{1,0:T(8,128)} %bitcast.5, ...), custom_call_target="tpu_custom_call" | custom-call | tf_op jit(solution)/shard_map/pallas_call | solution.py:337
  46.4 1.0 %shard_map.194 = (bf16[16,2048]{1,0:T(8,128)(2,1)}, bf16[16,32,4,128]{3,2,1,0:T(4,128)(2,1)}, bf16[16,32,4,128]{3,2,1,0:T(4,128)(2,1)}) custom-call(bf16[16,2048]{1,0:T(8,128)(2,1)S(1)} %get-tuple-element.6.a_ref, bf16[16,32,4,128]{3,2,1,0:T(4,128)(2,1)S(1)} %get-tuple-element.7.b_ref, bf16[16,32,4,128]{3,2,1,0:T(4,128)(2,1)S(1)} %get-tuple-element.8.c_ref), custom_call_target="tpu_custom_call" | custom-call | tf_op jit(solution)/shard_map/pallas_call | solution.py:359

commit v4 on v3

--- a/solution.py
+++ b/solution.py
@@ -22,7 +22,7 @@
 GQ = 8
 FF = 768
 CAP = 2
-GROUPS = ((0, 8), (8, 16))
+GROUPS = ((0, 4), (4, 8), (8, 12), (12, 16))
 GRP = len(GROUPS)
 MUL = 91
 STEP = 11
@@ -190,17 +190,19 @@
             pl.semaphore_wait(bar, N - 1)
         if g:
             at_copy(g - 1).start()
+    wo_copy(0).wait()
+    at_copy(0).wait()
+    yn = jnp.dot(at_v[0], wo_v[0], preferred_element_type=F32)
     attend(3, prev)
     at_copy(3).start()
-
-    yn = None
-    for g in range(NKV):
+    we_c[1].start()
+
+    for g in range(1, NKV):
         wo_copy(g).wait()
         at_copy(g).wait()
-        if g < 2:
-            we_c[g + 1].start()
-        part = jnp.dot(at_v[g], wo_v[g], preferred_element_type=F32)
-        yn = part if g == 0 else yn + part
+        if g == 1:
+            we_c[2].start()
+        yn = yn + jnp.dot(at_v[g], wo_v[g], preferred_element_type=F32)
     yh_v[half] = yn[0:S]
     yp_v[...] = yn[S:2 * S]
     ycp = pltpu.make_async_remote_copy(yp_v, yh_v.at[half], ys_sem, yr_sem, device_id={"ep": mate}, device_id_type=MESH)
@@ -297,16 +299,24 @@
             for j in range(4):
                 oview[n * 4 + j, r0:r1, :] = o[:, j * 128:(j + 1) * 128]
 
-        push_group(obuf, bbuf, osem, bsem, q, -1)
-    bbuf[:, 0] = obuf[:, 0]
-
-    got = bbuf.at[:, pl.ds(1, N - 1)]
-    cp(got, got, bsem).wait()
-    for n in range(4):
-        back = jnp.concatenate([bview[n * 4 + j] for j in range(4)], axis=1)
-        m = jnp.dot(g_v[...], back, preferred_element_type=F32)
-        cols = slice(n * 512, (n + 1) * 512)
-        out_ref[:, cols] = (y_v[:, cols] + (m[0:S] + m[S:2 * S] + m[2 * S:3 * S])).astype(BF)
+        push_group(obuf, bbuf, osem, bsem.at[q], q, -1)
+        if q == 0:
+            bbuf[:, 0] = obuf[:, 0]
+
+    for q in range(GRP):
+        lo, hi = max(1, GROUPS[q][0] * 8), GROUPS[q][1] * 8
+        r0, r1 = GROUPS[q][0] * 8 * CAP, hi * CAP
+        got = bbuf.at[:, pl.ds(lo, hi - lo)]
+        cp(got, got, bsem.at[q]).wait()
+        for n in range(4):
+            back = jnp.concatenate([bview[n * 4 + j, r0:r1, :] for j in range(4)], axis=1)
+            m = jnp.dot(g_v[:, r0:r1], back, preferred_element_type=F32)
+            cols = slice(n * 512, (n + 1) * 512)
+            tot = y_v[:, cols] + (m[0:S] + m[S:2 * S] + m[2 * S:3 * S])
+            if q + 1 < GRP:
+                y_v[:, cols] = tot
+            else:
+                out_ref[:, cols] = tot.astype(BF)
     sent = sbuf.at[:, pl.ds(1, N - 1)]
     cp(sent, sent, ssem).wait()
     cp(sent, sent, osem).wait()
@@ -350,7 +360,7 @@
                 V((CAP * N, FF), BF),
                 V((16, N, CAP, HD), BF), V((16, N, CAP, HD), BF), V((16, N, CAP, HD), BF), V((16, N, CAP, HD), BF),
                 dma((8,)), dma((2,)), dma((2,)), dma((4,)), dma((4,)), dma, dma((3,)), dma((4,)), dma((4,)), dma, dma,
-                dma, dma, dma((GRP,)), dma,
+                dma, dma, dma((GRP,)), dma((GRP,)),
             ],
             compiler_params=pltpu.CompilerParams(collective_id=0, has_side_effects=True, vmem_limit_bytes=60 * 1024 * 1024),
         )(hidden, k_cache, v_cache, seq_lens, expert_ids.T, ln_attn.reshape(16, 128), w_q, w_k, w_v,

time: 47.6 us -> 47.1 us (0.989)
  Pallas kernels: 46.8 us -> 46.3 us
    pallas_call x1, Pallas kernels: 45.8 us -> 45.3 us  [local_step(): pl.pallas_call(kernel, out_shape=(V((S, D), BF), V((S, T, NKV, HD), BF),...]
where the time goes in v4:
time: 47.1 us; the launch traced here: 47 us
  Pallas kernels  46.3 us (98%)
  between operations  0.65 us (1%)
    pallas_call x1, Pallas kernels, local_step(): pl.pallas_call(kernel, out_shape=(V((S, D), BF), V((S, T, NKV, HD), BF),...  45.3 us
    pallas_call x1, Pallas kernels, local_step(): pl.pallas_call(finish, out_shape=(jax.ShapeDtypeStruct((S, D), BF), jax.S...  1.02 us

profile of v4, /device:TPU:1, one launch (start us, length us, event | category | flops | bytes accessed | tf_op | source)
XLA Modules:
  0.0 47.0 jit_solution(3513806943589866750)
XLA Ops:
  0.6 45.3 %shard_map.193 = (bf16[16,2048]{1,0:T(8,128)(2,1)S(1)}, bf16[16,32,4,128]{3,2,1,0:T(4,128)(2,1)S(1)}, bf16[16,32,4,128]{3,2,1,0:T(4,128)(2,1)S(1)}) custom-call(bf16[16,2048]{1,0:T(8,128)(2,1)} %h_hbm.1, bf16[16,32,4,128]{3,2,1,0:T(4,128)(2,1)} %kc_hbm.1, bf16[16,32,4,128]{3,2,1,0:T(4,128)(2,1)} %vc_hbm.1, s32[16]{0:T(128)} %sl_hbm.1, s32[8,16]{1,0:T(8,128)} %bitcast.5, ...), custom_call_target="tpu_custom_call" | custom-call | tf_op jit(solution)/shard_map/pallas_call | solution.py:347
  45.9 1.0 %shard_map.194 = (bf16[16,2048]{1,0:T(8,128)(2,1)}, bf16[16,32,4,128]{3,2,1,0:T(4,128)(2,1)}, bf16[16,32,4,128]{3,2,1,0:T(4,128)(2,1)}) custom-call(bf16[16,2048]{1,0:T(8,128)(2,1)S(1)} %get-tuple-element.6.a_ref, bf16[16,32,4,128]{3,2,1,0:T(4,128)(2,1)S(1)} %get-tuple-element.7.b_ref, bf16[16,32,4,128]{3,2,1,0:T(4,128)(2,1)S(1)} %get-tuple-element.8.c_ref), custom_call_target="tpu_custom_call" | custom-call | tf_op jit(solution)/shard_map/pallas_call | solution.py:369

commit v5 on v4

--- a/solution.py
+++ b/solution.py
@@ -202,11 +202,17 @@
         at_copy(g).wait()
         if g == 1:
             we_c[2].start()
-        yn = yn + jnp.dot(at_v[g], wo_v[g], preferred_element_type=F32)
-    yh_v[half] = yn[0:S]
-    yp_v[...] = yn[S:2 * S]
-    ycp = pltpu.make_async_remote_copy(yp_v, yh_v.at[half], ys_sem, yr_sem, device_id={"ep": mate}, device_id_type=MESH)
-    ycp.start()
+        if g < NKV - 1:
+            yn = yn + jnp.dot(at_v[g], wo_v[g], preferred_element_type=F32)
+    ycps = []
+    for n in range(2):
+        cols = slice(n * 512, (n + 1) * 512)
+        yc = yn[:, cols] + jnp.dot(at_v[NKV - 1], wo_v[NKV - 1, :, cols], preferred_element_type=F32)
+        yh_v[half, :, cols] = yc[0:S]
+        yp_v[:, cols] = yc[S:2 * S]
+        ycps.append(pltpu.make_async_remote_copy(yp_v.at[:, pl.ds(n * 512, 512)], yh_v.at[half, :, pl.ds(n * 512, 512)],
+                                                 ys_sem.at[n], yr_sem.at[n], device_id={"ep": mate}, device_id_type=MESH))
+        ycps[n].start()
 
     mc, mx, my, mz = me % 2, me // 2 % 4, me // 8 % 4, me // 32
 
@@ -226,7 +232,8 @@
     snd_v[...] = jnp.transpose(send)
     p_v[...] = send.astype(BF)
 
-    ycp.wait()
+    for c in ycps:
+        c.wait()
     y = h_v[...].astype(F32) + jnp.concatenate([yh_v[0], yh_v[1]], axis=1)
     y_v[...] = y
     rs = lax.rsqrt(jnp.mean(y * y, axis=-1, keepdims=True) + EPS)
@@ -359,7 +366,7 @@
                 V((S, D), F32), V((S, D), BF), V((CAP * N, S), BF), V((S, CAP * N), F32), V((3 * S, CAP * N), BF),
                 V((CAP * N, FF), BF),
                 V((16, N, CAP, HD), BF), V((16, N, CAP, HD), BF), V((16, N, CAP, HD), BF), V((16, N, CAP, HD), BF),
-                dma((8,)), dma((2,)), dma((2,)), dma((4,)), dma((4,)), dma, dma((3,)), dma((4,)), dma((4,)), dma, dma,
+                dma((8,)), dma((2,)), dma((2,)), dma((4,)), dma((4,)), dma, dma((3,)), dma((4,)), dma((4,)), dma((2,)), dma((2,)),
                 dma, dma, dma((GRP,)), dma((GRP,)),
             ],
             compiler_params=pltpu.CompilerParams(collective_id=0, has_side_effects=True, vmem_limit_bytes=60 * 1024 * 1024),

time: 47.1 us -> 47.1 us (level)
  no operation moved by 1% of the time
where the time goes in v5:
time: 47.1 us; the launch traced here: 47 us
  Pallas kernels  46.4 us (99%)
  between operations  0.65 us (1%)
    pallas_call x1, Pallas kernels, local_step(): pl.pallas_call(kernel, out_shape=(V((S, D), BF), V((S, T, NKV, HD), BF),...  45.4 us
    pallas_call x1, Pallas kernels, local_step(): pl.pallas_call(finish, out_shape=(jax.ShapeDtypeStruct((S, D), BF), jax.S...  1.02 us

profile of v5, /device:TPU:1, one launch (start us, length us, event | category | flops | bytes accessed | tf_op | source)
XLA Modules:
  0.0 47.0 jit_solution(2211386587014398815)
XLA Ops:
  0.6 45.4 %shard_map.193 = (bf16[16,2048]{1,0:T(8,128)(2,1)S(1)}, bf16[16,32,4,128]{3,2,1,0:T(4,128)(2,1)S(1)}, bf16[16,32,4,128]{3,2,1,0:T(4,128)(2,1)S(1)}) custom-call(bf16[16,2048]{1,0:T(8,128)(2,1)} %h_hbm.1, bf16[16,32,4,128]{3,2,1,0:T(4,128)(2,1)} %kc_hbm.1, bf16[16,32,4,128]{3,2,1,0:T(4,128)(2,1)} %vc_hbm.1, s32[16]{0:T(128)} %sl_hbm.1, s32[8,16]{1,0:T(8,128)} %bitcast.5, ...), custom_call_target="tpu_custom_call" | custom-call | tf_op jit(solution)/shard_map/pallas_call | solution.py:354
  46.0 1.0 %shard_map.194 = (bf16[16,2048]{1,0:T(8,128)(2,1)}, bf16[16,32,4,128]{3,2,1,0:T(4,128)(2,1)}, bf16[16,32,4,128]{3,2,1,0:T(4,128)(2,1)}) custom-call(bf16[16,2048]{1,0:T(8,128)(2,1)S(1)} %get-tuple-element.6.a_ref, bf16[16,32,4,128]{3,2,1,0:T(4,128)(2,1)S(1)} %get-tuple-element.7.b_ref, bf16[16,32,4,128]{3,2,1,0:T(4,128)(2,1)S(1)} %get-tuple-element.8.c_ref), custom_call_target="tpu_custom_call" | custom-call | tf_op jit(solution)/shard_map/pallas_call | solution.py:376
